TPU v7x, 512 devices: a 4x2x32 block of a 4x8x32 slice. The times are simulated.
512 devices in a mesh: member: 2 (over y), lon: 32 (over z), lat: 8 (over x, core).
Axes of the slice: x: 4, y: 2, z: 32, core: 2. Of those that a mesh axis runs over, the one named last changes fastest.
The devices are a block of a 4x8x32 slice.
Arguments:
- tracer: float32 [64, 128, 4096], P('member', 'lat', 'lon'), parts along dimension 0, may hold values from -6 to 6
- velocity: float32 [2, 64, 128, 4096], P(None, 'member', 'lat', 'lon'), parts along dimension 1, may hold values from -0.9 to 0.9
- surface: float32 [256, 4096], P(('member', 'lat'), 'lon'), parts along dimension 0, may hold values from -6 to 6
- transport: float32 [4, 128, 4096], P('member', 'lat', 'lon'), parts along dimension 0, may hold values from -3 to 3
- horiz_mixing: float32 [64], P('member'), parts along dimension 0, may hold values from 0.03 to 0.2
- vert_mixing: float32 [62], P('member'), parts along dimension 0, may hold values from 0.3 to 30
- levels: int32 [128, 4096], P('lat', 'lon'), may hold values from 0 to 32, as said below
- land_tiles: int32 [8, 32], P('lat', 'lon'), may hold values 0 or 1
- fold_pair: int32 [4096], P('lon'), may hold values from 0 to 4095, as said below
Outputs:
- tracer_new: float32 [64, 128, 4096], P('member', 'lat', 'lon'), parts along dimension 0
- surface_new: float32 [256, 4096], P(('member', 'lat'), 'lon'), parts along dimension 0
- transport_new: float32 [4, 128, 4096], P('member', 'lat', 'lon'), parts along dimension 0
There are 2 independent parts, one for each index of `member`. A program takes and returns all parts, laid end to end along the dimension named above; an argument that names none is the same for every part. Nothing has to cross between parts.
Inputs may be any that keep to these rules, and one draw needn't show every extreme that they name: 0 marks a land cell, otherwise the count of sea levels. The fold pairing is a reflection: fold_pair[i] = (p - i) mod 4096 for one p in 0..4095, so fold_pair[fold_pair[i]] = i.
All inputs are finite; a program needn't handle non-finite values. No bound on the sum of `land_tiles` on one device may be relied on, other than what follows from the above.
Results may differ from a plain program's by a relative error of at most 0.00002.
Values sent between devices are 32-bit elements; how exact they have to be, the bound alone decides.
No kernel may reach another device: no remote copies, remote signals or barrier semaphores. Data moves between devices by JAX's collectives and lax.ppermute only.
A program may use at most 64 MiB of HBM per device.

v0:
```python
import functools

import jax
import jax.numpy as jnp
from jax import lax
from jax.experimental import pallas as pl
from jax.experimental.pallas import tpu as pltpu
from jax.sharding import PartitionSpec as P


SUB = 12
fb_step = 0.6
drag_rate = 0.02
EDGE = 16
F32 = jnp.float32


def lanes_of(shape):
    return lax.broadcasted_iota(jnp.int32, shape, 1)


def rows_of(shape):
    return lax.broadcasted_iota(jnp.int32, shape, 0)


def roll(x, shift, axis):
    return pltpu.roll(x, shift % x.shape[axis], axis)


def pack_kernel(land, tracer, velocity, surface, transport, levels, up, down, cols):
    depth, rows, width = tracer.shape
    real = (levels[...] * (1 - land[...])).astype(F32)
    for out, row in ((up, rows - 1), (down, 0)):
        out[0:rows] = surface[...]
        out[rows : 2 * rows] = transport[0]
        out[2 * rows : 3 * rows] = transport[1]
        out[3 * rows : 4 * rows] = real
        for k in range(depth):
            out[4 * rows + k : 4 * rows + k + 1] = tracer[k, row : row + 1]
            at = 4 * rows + depth + k
            out[at : at + 1] = velocity[1, k, row : row + 1]
    lane = lanes_of((8, width))
    first = jnp.zeros((8, width), F32)
    last = jnp.zeros((8, width), F32)
    spot = 0
    for field in range(2):
        for k in range(depth):
            for half in range(0, rows, 8):
                part = tracer[k, half : half + 8] if field == 0 else velocity[0, k, half : half + 8]
                first = jnp.where(lane == spot, part[:, :1], first)
                last = jnp.where(lane == spot, part[:, width - 1 :], last)
                spot += 1
    cols[0:8] = first
    cols[8:16] = last


def edge_kernel(lon, up, south, north, cols, main, extra, eastward, westward):
    rows = up.shape[0] // 8
    width = up.shape[1]
    groups = width // EDGE
    lane = lanes_of((8, width)) // EDGE
    n = 0
    east = west = None
    for field in range(4):
        for block in (south, up, north):
            for half in range(0, rows, 8):
                group = n % groups
                x = block[field * rows + half : field * rows + half + 8]
                to_east = roll(x, EDGE * group - (width - EDGE), 1)
                to_west = roll(x, EDGE * group, 1)
                if group == 0:
                    east, west = to_east, to_west
                else:
                    east = jnp.where(lane == group, to_east, east)
                    west = jnp.where(lane == group, to_west, west)
                n += 1
                if n % groups == 0:
                    at = 8 * (n // groups - 1)
                    eastward[at : at + 8] = east
                    westward[at : at + 8] = west
    at = 8 * (n // groups)
    eastward[at : at + 8] = cols[8:16]
    westward[at : at + 8] = cols[0:8]
    at, size = at + 8, main.shape[0]
    is_first = jnp.full((size, width), lon[0], jnp.int32) == 0
    eastward[at : at + size] = jnp.where(is_first, extra[...], main[...])
    westward[at : at + size] = main[...]
    westward[at + size : at + 2 * size] = extra[...]


def final_kernel(
    n_lon, lon_ref, turn_ref, top_ref, hmix, vmix, tracer, velocity, up, down, south, north, cols, from_west, from_east, main, extra,
    tracer_out, surface_out, transport_out,
    north_own, north_far, seam_own, seam_far, north_rows, primes,
):
    depth, rows, width = tracer.shape
    groups = width // EDGE
    lane8 = lanes_of((8, width))
    half_way = width // 2
    flat = 4 * rows

    def far_tile(n):
        at, group = 8 * (n // groups), n % groups
        east = roll(from_east[at : at + 8], -EDGE * group, 1)
        west = roll(from_west[at : at + 8], (width - EDGE) - EDGE * group, 1)
        return jnp.where(lane8 < half_way, east, west)

    def far_block(field, block):
        first = (field * 3 + block) * (rows // 8)
        return jnp.concatenate([far_tile(first + i) for i in range(rows // 8)], axis=0)

    def shifted(own, far, by):
        lane = lanes_of(own.shape)
        edge = width - 1 if by < 0 else 0
        a, b = roll(own, by, 1), roll(far, by, 1)
        return jnp.where(lane == edge, b, a), jnp.where(lane == edge, a, b)

    at_top = top_ref[0] == 1

    @pl.when(jnp.logical_not(at_top))
    def _():
        north_own[...] = north[0:flat]
        for field in range(4):
            north_far[field * rows : (field + 1) * rows] = far_block(field, 2)
        seam_own[...] = roll(up[3 * rows - 8 : 3 * rows], 1, 0)
        seam_far[...] = roll(far_tile((2 * 3 + 1) * (rows // 8) + rows // 8 - 1), 1, 0)
        north_rows[...] = north[flat : flat + 2 * depth]

    @pl.when(at_top)
    def _():
        turn = turn_ref[0]
        small = jnp.full((8, width), turn, jnp.int32) < half_way
        index = (turn - lane8) & (width - 1)
        less = lane8 <= turn
        back = 7 - rows_of((8, width))

        lon = jnp.full((8, width), lon_ref[0], jnp.int32)
        is_first, is_last = lon == 0, lon == n_lon - 1
        sent = 4 * 3 * rows // groups + 8
        size = main.shape[0]

        def pulled(at):
            mine, other = main[at : at + 8], extra[at : at + 8]
            west = from_west[sent + at : sent + at + 8]
            east = from_east[sent + at : sent + at + 8]
            further = from_east[sent + size + at : sent + size + at + 8]
            g0, g1, g2 = (
                jnp.take_along_axis(x, index, axis=1, mode="promise_in_bounds")
                for x in (
                    jnp.where(is_first, mine, west),
                    jnp.where(is_last, east, jnp.where(is_first, other, mine)),
                    jnp.where(is_last, further, jnp.where(is_first, east, other)),
                )
            )
            own = jnp.where(less, jnp.where(small, g0, g1), jnp.where(small, g1, g2))
            return own, g0, g1, g2

        def turned(x):
            return jnp.take_along_axis(x, back, axis=0, mode="promise_in_bounds")

        for field in range(4):
            own, far = [], []
            for half in range(rows - 8, -8, -8):
                mine, g0, g1, g2 = pulled(field * rows + half)
                low = jnp.where(jnp.logical_and(less, small), g1, g2)
                high = jnp.where(jnp.logical_or(less, small), g0, g1)
                own.append(turned(mine))
                far.append(turned(jnp.where(lane8 < half_way, low, high)))
            own, far = jnp.concatenate(own, axis=0), jnp.concatenate(far, axis=0)
            if field == 1:
                own, far = shifted(-own, -far, -1)
            if field == 2:
                seam_own[...] = -own[:8]
                seam_far[...] = -far[:8]
                own, far = roll(-own, -1, 0), roll(-far, -1, 0)
            north_own[field * rows : (field + 1) * rows] = own
            north_far[field * rows : (field + 1) * rows] = far
        for at in range(0, 2 * depth, 8):
            north_rows[at : at + 8] = pulled(flat + at)[0]

    def window(field):
        at = slice(field * rows, (field + 1) * rows)
        own = jnp.concatenate([south[at], up[at], north_own[at]], axis=0)
        far = jnp.concatenate([far_block(field, 0), far_block(field, 1), north_far[at]], axis=0)
        return own, far

    eta, far_eta = window(0)
    u, far_u = window(1)
    v, far_v = window(2)
    level, far_level = window(3)
    seam, far_seam = seam_own[...], seam_far[...]

    def sea_of(x):
        return (x > 0).astype(F32)

    sea, far_sea = sea_of(level), sea_of(far_level)
    east_sea, east_far_sea = shifted(sea, far_sea, -1)
    east_level, east_far_level = shifted(level, far_level, -1)
    scale = 2.0 * depth
    zmask, far_zmask = sea * east_sea, far_sea * east_far_sea
    zdepth = fb_step * ((level + east_level) / scale)
    far_zdepth = fb_step * ((far_level + east_far_level) / scale)
    mmask, far_mmask = sea * roll(sea, -1, 0), far_sea * roll(far_sea, -1, 0)
    mdepth = fb_step * ((level + roll(level, -1, 0)) / scale)
    far_mdepth = fb_step * ((far_level + roll(far_level, -1, 0)) / scale)
    cut = 2 * rows

    def below(x):
        return roll(x, 1, 0)[cut : cut + 8]

    seam_mask, far_seam_mask = below(mmask), below(far_mmask)
    seam_depth, far_seam_depth = below(mdepth), below(far_mdepth)
    row8 = rows_of((8, width))

    def south_of(x, line):
        moved = roll(x, 1, 0)
        fixed = jnp.where(row8 == 0, line, moved[cut : cut + 8])
        return jnp.concatenate([moved[:cut], fixed, moved[cut + 8 :]], axis=0)

    keep = 1.0 - drag_rate
    for _ in range(SUB):
        west_u, west_far_u = shifted(u, far_u, 1)
        div = (u - west_u) + (v - south_of(v, seam))
        far_div = (far_u - west_far_u) + (far_v - south_of(far_v, far_seam))
        eta = (eta - fb_step * div) * sea
        far_eta = (far_eta - fb_step * far_div) * far_sea
        east, far_east = shifted(eta, far_eta, -1)
        u = (u * keep - zdepth * (east - eta)) * zmask
        far_u = (far_u * keep - far_zdepth * (far_east - far_eta)) * far_zmask
        rise = eta[cut : cut + 8] - below(eta)
        far_rise = far_eta[cut : cut + 8] - below(far_eta)
        seam = (seam * keep - seam_depth * rise) * seam_mask
        far_seam = (far_seam * keep - far_seam_depth * far_rise) * far_seam_mask
        v = (v * keep - mdepth * (roll(eta, -1, 0) - eta)) * mmask
        far_v = (far_v * keep - far_mdepth * (roll(far_eta, -1, 0) - far_eta)) * far_mmask
    mid = slice(rows, 2 * rows)
    surface_out[...] = eta[mid]
    transport_out[0] = u[mid]
    transport_out[1] = v[mid]

    def face(near, beyond, wet_near, wet_beyond, vel_near, vel_beyond, mixing):
        flux = mixing * (beyond - near) - 0.25 * (vel_near + vel_beyond) * (near + beyond)
        return jnp.where(jnp.logical_and(wet_near, wet_beyond), flux, 0.0)

    level_row = rows_of((depth, width)).astype(F32)
    mix_rows = jnp.zeros((depth, width), F32)
    for k in range(depth):
        mix_rows = jnp.where(level_row == k, hmix[k], mix_rows)
    top, bottom = level[2 * rows - 1 : 2 * rows], level[rows : rows + 1]
    flux_top = face(
        up[flat : flat + depth],
        north_rows[0:depth],
        level_row < top,
        level_row < level[2 * rows : 2 * rows + 1],
        up[flat + depth : flat + 2 * depth],
        north_rows[depth : 2 * depth],
        mix_rows,
    )
    flux_bottom = face(
        south[flat : flat + depth],
        down[flat : flat + depth],
        level_row < level[rows - 1 : rows],
        level_row < bottom,
        south[flat + depth : flat + 2 * depth],
        down[flat + depth : flat + 2 * depth],
        mix_rows,
    )
    parts = rows // 8
    level_lane = ((lane8 & (parts * depth - 1)) // parts).astype(F32)
    mix_lanes = jnp.zeros((8, width), F32)
    for k in range(depth):
        mix_lanes = jnp.where(level_lane == k, hmix[k], mix_lanes)
    here, far_here = level[mid], far_level[mid]

    def column(x, at):
        packed = jnp.broadcast_to(x[:8, at : at + 1], (8, width))
        for i in range(1, parts):
            packed = jnp.where(lane8 % parts == i, x[8 * i : 8 * i + 8, at : at + 1], packed)
        return packed

    def side(near, beyond, level_near, level_beyond):
        return face(
            near,
            beyond,
            level_lane < level_near,
            level_lane < level_beyond,
            roll(near, -half_way, 1),
            roll(beyond, -half_way, 1),
            mix_lanes,
        )

    spot = 8 * (4 * 3 * parts // groups)
    flux_right = side(
        cols[8:16], from_east[spot : spot + 8], column(here, width - 1), column(far_here, 0)
    )
    flux_left = side(
        from_west[spot : spot + 8], cols[0:8], column(far_here, width - 1), column(here, 0)
    )

    lane = lanes_of((rows, width))
    row = rows_of((rows, width))
    here_east = roll(here, -1, 1)
    here_north = roll(here, -1, 0)

    def spread(x, k):
        return jnp.concatenate(
            [jnp.broadcast_to(x[:, parts * k + i : parts * k + i + 1], (8, width)) for i in range(parts)],
            axis=0,
        )

    sweep = prime = link = None
    for k in range(depth):
        field, zonal, merid = tracer[k], velocity[0, k], velocity[1, k]
        wet = here > k
        mixing = hmix[k]
        east_flux = face(
            field, roll(field, -1, 1), wet, here_east > k, zonal, roll(zonal, -1, 1), mixing
        )
        east_flux = jnp.where(lane == width - 1, spread(flux_right, k), east_flux)
        west_flux = jnp.where(lane == 0, spread(flux_left, k), roll(east_flux, 1, 1))
        north_flux = face(
            field, roll(field, -1, 0), wet, here_north > k, merid, roll(merid, -1, 0), mixing
        )
        north_flux = jnp.where(row == rows - 1, flux_top[k : k + 1], north_flux)
        south_flux = jnp.where(row == 0, flux_bottom[k : k + 1], roll(north_flux, 1, 0))
        stepped = jnp.where(
            wet, field + ((east_flux - west_flux) + (north_flux - south_flux)), 0.0
        )
        diagonal = jnp.ones_like(stepped)
        if k > 0:
            diagonal = diagonal + link
        if k < depth - 1:
            next_link = jnp.where(here > k + 1, vmix[k], 0.0)
            diagonal = diagonal + next_link
        if k > 0:
            diagonal = diagonal + link * prime
            stepped = stepped + link * sweep
        inverse = 1.0 / diagonal
        sweep = stepped * inverse
        tracer_out[k] = sweep
        if k < depth - 1:
            prime = -next_link * inverse
            primes[k] = prime
            link = next_link
    solved = sweep
    for k in range(depth - 2, -1, -1):
        solved = tracer_out[k] - primes[k] * solved
        tracer_out[k] = solved


def shards(
    tracer, velocity, surface, transport, horiz_mixing, vert_mixing, levels, land_tiles, fold_pair,
    *, n_lon, n_lat, interpret,
):
    depth, rows, width = tracer.shape
    smem = pl.BlockSpec(memory_space=pltpu.SMEM)
    vmem = pl.BlockSpec(memory_space=pltpu.VMEM)
    call = functools.partial(pl.pallas_call, interpret=interpret)

    def like(*shape):
        return jax.ShapeDtypeStruct(shape, F32)

    stack = 4 * rows + 2 * depth
    up, down, cols = call(
        pack_kernel,
        out_shape=(like(stack, width), like(stack, width), like(16, width)),
        in_specs=[vmem] * 6,
        out_specs=(vmem,) * 3,
        name="pack",
    )(land_tiles, tracer, velocity, surface, transport, levels)

    south = lax.ppermute(up, "lat", [(i, i + 1) for i in range(n_lat - 1)])
    north = lax.ppermute(down, "lat", [(i + 1, i) for i in range(n_lat - 1)])

    lon = lax.axis_index("lon")
    pivot = (fold_pair[0] + width * lon) % (width * n_lon)
    turn = pivot % width
    tile = (pivot // width - (turn < width // 2).astype(jnp.int32)) % n_lon

    def fetch(x, shift):
        routes = [(shift + 1, 0)] + [(shift - t, t) for t in range(1, n_lon - 1)]
        pairs = [(s % n_lon * n_lat + n_lat - 1, t * n_lat + n_lat - 1) for s, t in routes]
        return lax.ppermute(x, ("lon", "lat"), pairs)

    def branch(shift):
        return lambda x: (fetch(x, shift), fetch(x, (shift - 1) % n_lon))

    main, extra = lax.switch(tile, [branch(shift) for shift in range(n_lon)], up)

    at_top = (lax.axis_index("lat") == n_lat - 1).astype(jnp.int32)
    lon, turn, at_top = (x.reshape(1) for x in (lon, turn, at_top))
    edge_rows = 4 * 3 * rows * EDGE // width + 8
    eastward, westward = call(
        edge_kernel,
        out_shape=(like(edge_rows + stack, width), like(edge_rows + 2 * stack, width)),
        in_specs=[smem] + [vmem] * 6,
        out_specs=(vmem,) * 2,
        name="edge",
    )(lon, up, south, north, cols, main, extra)
    from_west = lax.ppermute(eastward, "lon", [(i, (i + 1) % n_lon) for i in range(n_lon)])
    from_east = lax.ppermute(westward, "lon", [((i + 1) % n_lon, i) for i in range(n_lon)])

    return call(
        functools.partial(final_kernel, n_lon),
        out_shape=(like(depth, rows, width), like(rows, width), like(2, rows, width)),
        in_specs=[smem] * 5 + [vmem] * 11,
        out_specs=(vmem,) * 3,
        scratch_shapes=[
            pltpu.VMEM((4 * rows, width), F32),
            pltpu.VMEM((4 * rows, width), F32),
            pltpu.VMEM((8, width), F32),
            pltpu.VMEM((8, width), F32),
            pltpu.VMEM((2 * depth, width), F32),
            pltpu.VMEM((depth, rows, width), F32),
        ],
        name="final",
    )(
        lon, turn, at_top, horiz_mixing, vert_mixing, tracer, velocity, up, down, south, north, cols,
        from_west, from_east, main, extra,
    )


def solution(mesh, interpret=False):
    def step(*args):
        return shards(*args, n_lon=mesh.shape["lon"], n_lat=mesh.shape["lat"], interpret=interpret)

    return jax.shard_map(
        step,
        mesh=mesh,
        in_specs=(
            P("member", "lat", "lon"),
            P(None, "member", "lat", "lon"),
            P(("member", "lat"), "lon"),
            P("member", "lat", "lon"),
            P("member"),
            P("member"),
            P("lat", "lon"),
            P("lat", "lon"),
            P("lon"),
        ),
        out_specs=(
            P("member", "lat", "lon"),
            P(("member", "lat"), "lon"),
            P("member", "lat", "lon"),
        ),
        check_vma=False,
    )
```

profile of v0, /device:TPU:39, one launch (start us, length us, event | category | flops | bytes accessed | tf_op | source)
XLA Modules:
  0.0 85.2 jit_solution(12167322980580917350)
XLA Ops:
  1.3 2.2 %pack.1 = (f32[128,128]{1,0:T(8,128)S(1)}, f32[128,128]{1,0:T(8,128)}, f32[16,128]{1,0:T(8,128)}) custom-call(s32[1,1]{1,0:T(1,128)S(6)} %copy.76.land, f32[32,16,128]{2,1,0:T(8,128)} %tracer.3, f32[2,32,16,128]{3,2,1,0:T(8,128)} %velocity.3, f32[16,128]{1,0:T(8,128)} %surface.1, f32[2,16,128]{2,1,0:T(8,128)} %transport.1, s32[16,128]{1,0:T(8,128)} %levels.1), custom_call_target="tpu_custom_call" | custom-call | tf_op jit(solution)/shard_map/pack/pallas_call | solution.py:364
  3.5 2.5 %collective-permute-start.65 = (f32[128,128]{1,0:T(8,128)}, f32[128,128]{1,0:T(8,128)S(1)}, u32[]{:S(2)}, u32[]{:S(2)}) collective-permute-start(f32[128,128]{1,0:T(8,128)} %get-tuple-element.43.down), channel_id=1, source_target_pairs={{1,0},{2,1},{3,2},{4,3},{5,4},{6,5},{7,6},{9,8},{10,9},{11,10},{12... | collective-permute-start | bytes 196616 | tf_op jit(solution)/shard_map/ppermute | solution.py:373
  6.0 1.3 %collective-permute-start.64 = (f32[128,128]{1,0:T(8,128)S(1)}, f32[128,128]{1,0:T(8,128)S(1)}, u32[]{:S(2)}, u32[]{:S(2)}) collective-permute-start(f32[128,128]{1,0:T(8,128)S(1)} %get-tuple-element.42.up), channel_id=1, source_target_pairs={{0,1},{1,2},{2,3},{3,4},{4,5},{5,6},{6,7},{8,9},{9,10},{10,11},{11... | collective-permute-start | bytes 196616 | tf_op jit(solution)/shard_map/ppermute | solution.py:372
  7.4 0.0 copy-start.4
  7.4 0.6 copy-done.4
  8.1 59.3 %conditional.1 = (f32[128,128]{1,0:T(8,128)}, f32[128,128]{1,0:T(8,128)}) conditional(s32[]{:T(128)} %clamp.3, f32[128,128]{1,0:T(8,128)S(1)} %get-tuple-element.42.up, f32[128,128]{1,0:T(8,128)S(1)} %get-tuple-element.42.up, f32[128,128]{1,0:T(8,128)S(1)} %get-tuple-element.42.up, ...), branch_computations={%region_0.1_spmd, %region_1.2_spmd, %region_2.3_spmd, %region_3.4_... | conditional | bytes 524384 | solution.py:388
  8.2 6.6 %collective-permute-start.7 = (f32[128,128]{1,0:T(8,128)S(1)}, f32[128,128]{1,0:T(8,128)}, u32[]{:S(2)}, u32[]{:S(2)}) collective-permute-start(f32[128,128]{1,0:T(8,128)S(1)} %param.3), channel_id=1, source_target_pairs={{31,7},{15,15},{7,23},{255,31},{247,39},{239,47},{231,55},{223,63}... | collective-permute-start | bytes 196616 | tf_op jit(solution)/shard_map/cond/branch_3_fun/ppermute | solution.py:383
  14.8 4.2 %collective-permute-start.6 = (f32[128,128]{1,0:T(8,128)S(1)}, f32[128,128]{1,0:T(8,128)}, u32[]{:S(2)}, u32[]{:S(2)}) collective-permute-start(f32[128,128]{1,0:T(8,128)S(1)} %param.3), channel_id=1, source_target_pairs={{39,7},{23,15},{15,23},{7,31},{255,39},{247,47},{239,55},{231,63},... | collective-permute-start | bytes 196616 | tf_op jit(solution)/shard_map/cond/branch_3_fun/ppermute | solution.py:383
  19.0 0.0 collective-permute-done.7
  19.0 48.5 %collective-permute-done.6 = f32[128,128]{1,0:T(8,128)} collective-permute-done((f32[128,128]{1,0:T(8,128)S(1)}, f32[128,128]{1,0:T(8,128)}, u32[]{:S(2)}, u32[]{:S(2)}) %collective-permute-start.6) | collective-permute-done | bytes 65568 | tf_op jit(solution)/shard_map/cond/branch_3_fun/ppermute | solution.py:383
  67.5 0.0 collective-permute-done.65.north
  67.5 0.0 copy-start
  67.5 0.0 collective-permute-done.64.south
  67.5 0.0 copy-start.1
  67.5 0.6 copy-done
  68.1 0.0 copy-done.1
  68.1 1.7 %edge.1 = (f32[160,128]{1,0:T(8,128)}, f32[288,128]{1,0:T(8,128)}) custom-call(s32[1]{0:T(128)} %bitcast.lon.lon_ref, f32[128,128]{1,0:T(8,128)S(1)} %get-tuple-element.42.up, f32[128,128]{1,0:T(8,128)} %copy-done.1, f32[128,128]{1,0:T(8,128)} %copy-done, f32[16,128]{1,0:T(8,128)} %get-tuple-element.44.cols, f32[128,128]{1,0:T(8,128)} %get-tuple-element.45.main, ...), custom_call_target="tpu_custom_call" | custom-call | tf_op jit(solution)/shard_map/edge/pallas_call | solution.py:393
  69.8 1.9 %collective-permute-start.67 = (f32[288,128]{1,0:T(8,128)}, f32[288,128]{1,0:T(8,128)S(1)}, u32[]{:S(2)}, u32[]{:S(2)}) collective-permute-start(f32[288,128]{1,0:T(8,128)} %get-tuple-element.48), channel_id=1, source_target_pairs={{8,0},{16,8},{24,16},{32,24},{40,32},{48,40},{56,48},{64,56},{72,6... | collective-permute-start | bytes 442376 | tf_op jit(solution)/shard_map/ppermute | solution.py:401
  71.8 3.4 %collective-permute-start.66 = (f32[160,128]{1,0:T(8,128)}, f32[160,128]{1,0:T(8,128)S(1)}, u32[]{:S(2)}, u32[]{:S(2)}) collective-permute-start(f32[160,128]{1,0:T(8,128)} %get-tuple-element.47), channel_id=1, source_target_pairs={{0,8},{8,16},{16,24},{24,32},{32,40},{40,48},{48,56},{56,64},{64,7... | collective-permute-start | bytes 245768 | tf_op jit(solution)/shard_map/ppermute | solution.py:400
  75.2 4.0 %collective-permute-done.66.from_west = f32[160,128]{1,0:T(8,128)S(1)} collective-permute-done((f32[160,128]{1,0:T(8,128)}, f32[160,128]{1,0:T(8,128)S(1)}, u32[]{:S(2)}, u32[]{:S(2)}) %collective-permute-start.66) | collective-permute-done | bytes 81952 | tf_op jit(solution)/shard_map/ppermute | solution.py:400
  79.2 0.0 copy-start.3
  79.2 0.0 collective-permute-done.67.from_east
  79.2 0.0 copy-start.2
  79.2 0.6 copy-done.3
  79.8 0.1 copy-done.2
  79.9 5.3 %final.1 = (f32[32,16,128]{2,1,0:T(8,128)}, f32[16,128]{1,0:T(8,128)}, f32[2,16,128]{2,1,0:T(8,128)}) custom-call(s32[1]{0:T(128)} %bitcast.lon.lon_ref, s32[1]{0:T(128)} %bitcast.2.turn_ref, s32[1]{0:T(128)} %bitcast.3.top_ref, f32[32]{0:T(128)} %hmix.1, f32[31]{0:T(128)} %vmix.1, f32[32,16,128]{2,1,0:T(8,128)} %tracer.3, f32[2,32,16,128]{3,2,1,0:T(8,128)} %velocity.3, ...), custom_call_target="tpu_custom_call" | custom-call | tf_op jit(solution)/shard_map/final/pallas_call | solution.py:403
Async XLA Ops:
  3.5 64.0 %collective-permute-start.65 = (f32[128,128]{1,0:T(8,128)}, f32[128,128]{1,0:T(8,128)S(1)}, u32[]{:S(2)}, u32[]{:S(2)}) collective-permute-start(f32[128,128]{1,0:T(8,128)} %get-tuple-element.43.down), channel_id=1, source_target_pairs={{1,0},{2,1},{3,2},{4,3},{5,4},{6,5},{7,6},{9,8},{10,9},{11,10},{12... | collective-permute-start | bytes 196616 | tf_op jit(solution)/shard_map/ppermute | solution.py:373
  6.0 61.4 %collective-permute-start.64 = (f32[128,128]{1,0:T(8,128)S(1)}, f32[128,128]{1,0:T(8,128)S(1)}, u32[]{:S(2)}, u32[]{:S(2)}) collective-permute-start(f32[128,128]{1,0:T(8,128)S(1)} %get-tuple-element.42.up), channel_id=1, source_target_pairs={{0,1},{1,2},{2,3},{3,4},{4,5},{5,6},{6,7},{8,9},{9,10},{10,11},{11... | collective-permute-start | bytes 196616 | tf_op jit(solution)/shard_map/ppermute | solution.py:372
  7.4 0.7 copy-start.4
  8.2 10.8 %collective-permute-start.7 = (f32[128,128]{1,0:T(8,128)S(1)}, f32[128,128]{1,0:T(8,128)}, u32[]{:S(2)}, u32[]{:S(2)}) collective-permute-start(f32[128,128]{1,0:T(8,128)S(1)} %param.3), channel_id=1, source_target_pairs={{31,7},{15,15},{7,23},{255,31},{247,39},{239,47},{231,55},{223,63}... | collective-permute-start | bytes 196616 | tf_op jit(solution)/shard_map/cond/branch_3_fun/ppermute | solution.py:383
  14.8 52.6 %collective-permute-start.6 = (f32[128,128]{1,0:T(8,128)S(1)}, f32[128,128]{1,0:T(8,128)}, u32[]{:S(2)}, u32[]{:S(2)}) collective-permute-start(f32[128,128]{1,0:T(8,128)S(1)} %param.3), channel_id=1, source_target_pairs={{39,7},{23,15},{15,23},{7,31},{255,39},{247,47},{239,55},{231,63},... | collective-permute-start | bytes 196616 | tf_op jit(solution)/shard_map/cond/branch_3_fun/ppermute | solution.py:383
  67.5 0.6 copy-start
  67.5 0.6 copy-start.1
  69.8 9.3 %collective-permute-start.67 = (f32[288,128]{1,0:T(8,128)}, f32[288,128]{1,0:T(8,128)S(1)}, u32[]{:S(2)}, u32[]{:S(2)}) collective-permute-start(f32[288,128]{1,0:T(8,128)} %get-tuple-element.48), channel_id=1, source_target_pairs={{8,0},{16,8},{24,16},{32,24},{40,32},{48,40},{56,48},{64,56},{72,6... | collective-permute-start | bytes 442376 | tf_op jit(solution)/shard_map/ppermute | solution.py:401
  71.8 7.4 %collective-permute-start.66 = (f32[160,128]{1,0:T(8,128)}, f32[160,128]{1,0:T(8,128)S(1)}, u32[]{:S(2)}, u32[]{:S(2)}) collective-permute-start(f32[160,128]{1,0:T(8,128)} %get-tuple-element.47), channel_id=1, source_target_pairs={{0,8},{8,16},{16,24},{24,32},{32,40},{40,48},{48,56},{56,64},{64,7... | collective-permute-start | bytes 245768 | tf_op jit(solution)/shard_map/ppermute | solution.py:400
  79.2 0.6 copy-start.3
  79.2 0.7 copy-start.2
where the time goes:
time: 85.5 us; the launch traced here: 85.2 us
  waiting for transfers between devices  52.5 us (61%)
  starting transfers between devices  20 us (23%)
  Pallas kernels  9.3 us (11%)
  local copies, waits for them, and re-layouts  1.96 us (2%)
  between operations  1.45 us (2%)
    ppermute x2, waiting for transfers between devices, fetch(): return lax.ppermute(x, ('lon', 'lat'), pairs)  48.5 us
    ppermute x2, starting transfers between devices, fetch(): return lax.ppermute(x, ('lon', 'lat'), pairs)  10.8 us
    pallas_call x1, Pallas kernels, shards(): call(functools.partial(final_kernel, n_lon), out_shape=(like(depth, rows,...  5.32 us
    ppermute x1, waiting for transfers between devices, shards(): lax.ppermute(eastward, 'lon', [(i, (i + 1) % n_lon) for i in range(n_lon)])  3.99 us
    ppermute x1, starting transfers between devices, shards(): lax.ppermute(eastward, 'lon', [(i, (i + 1) % n_lon) for i in range(n_lon)])  3.39 us
    ppermute x1, starting transfers between devices, shards(): north = lax.ppermute(down, 'lat', [(i + 1, i) for i in range(n_lat - 1)])  2.53 us
    pallas_call x1, Pallas kernels, shards(): call(pack_kernel, out_shape=(like(stack, width), like(stack, width), like...  2.23 us
    unnamed x10, local copies, waits for them, and re-layouts  1.96 us
  transfers between devices with their start and end apart: 6, of which 2 were waited for; matrix products, arithmetic and copies ran while one was open for 0% of the time, Pallas kernels for 0%

commit v1 on v0

--- a/solution.py
+++ b/solution.py
@@ -383,9 +383,13 @@
         return lax.ppermute(x, ("lon", "lat"), pairs)
 
     def branch(shift):
-        return lambda x: (fetch(x, shift), fetch(x, (shift - 1) % n_lon))
-
-    main, extra = lax.switch(tile, [branch(shift) for shift in range(n_lon)], up)
+        def both(x):
+            later = fetch(x, (shift - 1) % n_lon)
+            return later, fetch(x, shift)
+
+        return both
+
+    extra, main = lax.switch(tile, [branch(shift) for shift in range(n_lon)], up)
 
     at_top = (lax.axis_index("lat") == n_lat - 1).astype(jnp.int32)
     lon, turn, at_top = (x.reshape(1) for x in (lon, turn, at_top))

time: 85.5 us -> 85.9 us (level)
  starting transfers between devices: 20 us -> 52.6 us
  waiting for transfers between devices: 52.5 us -> 20.2 us
    ppermute x2, waiting for transfers between devices: 48.5 us -> 5.09 us  [fetch(): return lax.ppermute(x, ('lon', 'lat'), pairs)]
    ppermute x1, starting transfers between devices: 1.94 us -> 35.9 us  [shards(): lax.ppermute(westward, 'lon', [((i + 1) % n_lon, i) for i in range(n_lon)])]
    ppermute x1, waiting for transfers between devices: 3.99 us -> 15.1 us  [shards(): lax.ppermute(eastward, 'lon', [(i, (i + 1) % n_lon) for i in range(n_lon)])]
    ppermute x1, starting transfers between devices: 3.39 us -> 1.95 us  [shards(): lax.ppermute(eastward, 'lon', [(i, (i + 1) % n_lon) for i in range(n_lon)])]
  transfers between devices with their start and end apart: 6 -> 6, of which waited for: 2 -> 3; matrix products, arithmetic and copies ran while one was open for 0% -> 0% of each run, Pallas kernels for 0% -> 0%
where the time goes in v1:
time: 85.9 us; the launch traced here: 85.5 us
  starting transfers between devices  52.6 us (61%)
  waiting for transfers between devices  20.2 us (24%)
  Pallas kernels  9.3 us (11%)
  local copies, waits for them, and re-layouts  1.96 us (2%)
  between operations  1.45 us (2%)
    ppermute x1, starting transfers between devices, shards(): lax.ppermute(westward, 'lon', [((i + 1) % n_lon, i) for i in range(n_lon)])  35.9 us
    ppermute x1, waiting for transfers between devices, shards(): lax.ppermute(eastward, 'lon', [(i, (i + 1) % n_lon) for i in range(n_lon)])  15.1 us
    ppermute x2, starting transfers between devices, fetch(): return lax.ppermute(x, ('lon', 'lat'), pairs)  10.8 us
    pallas_call x1, Pallas kernels, shards(): call(functools.partial(final_kernel, n_lon), out_shape=(like(depth, rows,...  5.32 us
    ppermute x2, waiting for transfers between devices, fetch(): return lax.ppermute(x, ('lon', 'lat'), pairs)  5.09 us
    ppermute x1, starting transfers between devices, shards(): north = lax.ppermute(down, 'lat', [(i + 1, i) for i in range(n_lat - 1)])  2.53 us
    pallas_call x1, Pallas kernels, shards(): call(pack_kernel, out_shape=(like(stack, width), like(stack, width), like...  2.23 us
    unnamed x10, local copies, waits for them, and re-layouts  1.96 us
  transfers between devices with their start and end apart: 6, of which 3 were waited for; matrix products, arithmetic and copies ran while one was open for 0% of the time, Pallas kernels for 0%

profile of v1, /device:TPU:39, one launch (start us, length us, event | category | flops | bytes accessed | tf_op | source)
XLA Modules:
  0.0 85.5 jit_solution(15766225629000816477)
XLA Ops:
  1.3 2.2 %pack.1 = (f32[128,128]{1,0:T(8,128)S(1)}, f32[128,128]{1,0:T(8,128)}, f32[16,128]{1,0:T(8,128)}) custom-call(s32[1,1]{1,0:T(1,128)S(6)} %copy.76.land, f32[32,16,128]{2,1,0:T(8,128)} %tracer.3, f32[2,32,16,128]{3,2,1,0:T(8,128)} %velocity.3, f32[16,128]{1,0:T(8,128)} %surface.1, f32[2,16,128]{2,1,0:T(8,128)} %transport.1, s32[16,128]{1,0:T(8,128)} %levels.1), custom_call_target="tpu_custom_call" | custom-call | tf_op jit(solution)/shard_map/pack/pallas_call | solution.py:364
  3.5 2.5 %collective-permute-start.65 = (f32[128,128]{1,0:T(8,128)}, f32[128,128]{1,0:T(8,128)S(1)}, u32[]{:S(2)}, u32[]{:S(2)}) collective-permute-start(f32[128,128]{1,0:T(8,128)} %get-tuple-element.43.down), channel_id=1, source_target_pairs={{1,0},{2,1},{3,2},{4,3},{5,4},{6,5},{7,6},{9,8},{10,9},{11,10},{12... | collective-permute-start | bytes 196616 | tf_op jit(solution)/shard_map/ppermute | solution.py:373
  6.0 1.3 %collective-permute-start.64 = (f32[128,128]{1,0:T(8,128)S(1)}, f32[128,128]{1,0:T(8,128)S(1)}, u32[]{:S(2)}, u32[]{:S(2)}) collective-permute-start(f32[128,128]{1,0:T(8,128)S(1)} %get-tuple-element.42.up), channel_id=1, source_target_pairs={{0,1},{1,2},{2,3},{3,4},{4,5},{5,6},{6,7},{8,9},{9,10},{10,11},{11... | collective-permute-start | bytes 196616 | tf_op jit(solution)/shard_map/ppermute | solution.py:372
  7.4 0.0 copy-start.4
  7.4 0.6 copy-done.4
  8.1 15.9 %conditional.1 = (f32[128,128]{1,0:T(8,128)}, f32[128,128]{1,0:T(8,128)}) conditional(s32[]{:T(128)} %clamp.3, f32[128,128]{1,0:T(8,128)S(1)} %get-tuple-element.42.up, f32[128,128]{1,0:T(8,128)S(1)} %get-tuple-element.42.up, f32[128,128]{1,0:T(8,128)S(1)} %get-tuple-element.42.up, ...), branch_computations={%region_0.1_spmd, %region_1.2_spmd, %region_2.3_spmd, %region_3.4_... | conditional | bytes 524384 | solution.py:392
  8.2 8.9 %collective-permute-start.7 = (f32[128,128]{1,0:T(8,128)S(1)}, f32[128,128]{1,0:T(8,128)}, u32[]{:S(2)}, u32[]{:S(2)}) collective-permute-start(f32[128,128]{1,0:T(8,128)S(1)} %param.3), channel_id=1, source_target_pairs={{39,7},{23,15},{15,23},{7,31},{255,39},{247,47},{239,55},{231,63},... | collective-permute-start | bytes 196616 | tf_op jit(solution)/shard_map/cond/branch_3_fun/ppermute | solution.py:383
  17.0 2.0 %collective-permute-start.6 = (f32[128,128]{1,0:T(8,128)S(1)}, f32[128,128]{1,0:T(8,128)}, u32[]{:S(2)}, u32[]{:S(2)}) collective-permute-start(f32[128,128]{1,0:T(8,128)S(1)} %param.3), channel_id=1, source_target_pairs={{31,7},{15,15},{7,23},{255,31},{247,39},{239,47},{231,55},{223,63}... | collective-permute-start | bytes 196616 | tf_op jit(solution)/shard_map/cond/branch_3_fun/ppermute | solution.py:383
  19.0 3.3 %collective-permute-done.7 = f32[128,128]{1,0:T(8,128)} collective-permute-done((f32[128,128]{1,0:T(8,128)S(1)}, f32[128,128]{1,0:T(8,128)}, u32[]{:S(2)}, u32[]{:S(2)}) %collective-permute-start.7) | collective-permute-done | bytes 65568 | tf_op jit(solution)/shard_map/cond/branch_3_fun/ppermute | solution.py:383
  22.3 1.8 %collective-permute-done.6 = f32[128,128]{1,0:T(8,128)} collective-permute-done((f32[128,128]{1,0:T(8,128)S(1)}, f32[128,128]{1,0:T(8,128)}, u32[]{:S(2)}, u32[]{:S(2)}) %collective-permute-start.6) | collective-permute-done | bytes 65568 | tf_op jit(solution)/shard_map/cond/branch_3_fun/ppermute | solution.py:383
  24.1 0.0 collective-permute-done.65.north
  24.1 0.0 copy-start
  24.1 0.0 collective-permute-done.64.south
  24.1 0.0 copy-start.1
  24.1 0.6 copy-done
  24.7 0.0 copy-done.1
  24.7 1.7 %edge.1 = (f32[160,128]{1,0:T(8,128)}, f32[288,128]{1,0:T(8,128)}) custom-call(s32[1]{0:T(128)} %bitcast.lon.lon_ref, f32[128,128]{1,0:T(8,128)S(1)} %get-tuple-element.42.up, f32[128,128]{1,0:T(8,128)} %copy-done.1, f32[128,128]{1,0:T(8,128)} %copy-done, f32[16,128]{1,0:T(8,128)} %get-tuple-element.44.cols, f32[128,128]{1,0:T(8,128)} %get-tuple-element.45.main, ...), custom_call_target="tpu_custom_call" | custom-call | tf_op jit(solution)/shard_map/edge/pallas_call | solution.py:397
  26.5 35.9 %collective-permute-start.67 = (f32[288,128]{1,0:T(8,128)}, f32[288,128]{1,0:T(8,128)S(1)}, u32[]{:S(2)}, u32[]{:S(2)}) collective-permute-start(f32[288,128]{1,0:T(8,128)} %get-tuple-element.48), channel_id=1, source_target_pairs={{8,0},{16,8},{24,16},{32,24},{40,32},{48,40},{56,48},{64,56},{72,6... | collective-permute-start | bytes 442376 | tf_op jit(solution)/shard_map/ppermute | solution.py:405
  62.4 2.0 %collective-permute-start.66 = (f32[160,128]{1,0:T(8,128)}, f32[160,128]{1,0:T(8,128)S(1)}, u32[]{:S(2)}, u32[]{:S(2)}) collective-permute-start(f32[160,128]{1,0:T(8,128)} %get-tuple-element.47), channel_id=1, source_target_pairs={{0,8},{8,16},{16,24},{24,32},{32,40},{40,48},{48,56},{56,64},{64,7... | collective-permute-start | bytes 245768 | tf_op jit(solution)/shard_map/ppermute | solution.py:404
  64.4 15.1 %collective-permute-done.66.from_west = f32[160,128]{1,0:T(8,128)S(1)} collective-permute-done((f32[160,128]{1,0:T(8,128)}, f32[160,128]{1,0:T(8,128)S(1)}, u32[]{:S(2)}, u32[]{:S(2)}) %collective-permute-start.66) | collective-permute-done | bytes 81952 | tf_op jit(solution)/shard_map/ppermute | solution.py:404
  79.5 0.0 copy-start.3
  79.5 0.0 collective-permute-done.67.from_east
  79.5 0.0 copy-start.2
  79.5 0.6 copy-done.3
  80.2 0.1 copy-done.2
  80.2 5.3 %final.1 = (f32[32,16,128]{2,1,0:T(8,128)}, f32[16,128]{1,0:T(8,128)}, f32[2,16,128]{2,1,0:T(8,128)}) custom-call(s32[1]{0:T(128)} %bitcast.lon.lon_ref, s32[1]{0:T(128)} %bitcast.2.turn_ref, s32[1]{0:T(128)} %bitcast.3.top_ref, f32[32]{0:T(128)} %hmix.1, f32[31]{0:T(128)} %vmix.1, f32[32,16,128]{2,1,0:T(8,128)} %tracer.3, f32[2,32,16,128]{3,2,1,0:T(8,128)} %velocity.3, ...), custom_call_target="tpu_custom_call" | custom-call | tf_op jit(solution)/shard_map/final/pallas_call | solution.py:407
Async XLA Ops:
  3.5 20.6 %collective-permute-start.65 = (f32[128,128]{1,0:T(8,128)}, f32[128,128]{1,0:T(8,128)S(1)}, u32[]{:S(2)}, u32[]{:S(2)}) collective-permute-start(f32[128,128]{1,0:T(8,128)} %get-tuple-element.43.down), channel_id=1, source_target_pairs={{1,0},{2,1},{3,2},{4,3},{5,4},{6,5},{7,6},{9,8},{10,9},{11,10},{12... | collective-permute-start | bytes 196616 | tf_op jit(solution)/shard_map/ppermute | solution.py:373
  6.0 18.0 %collective-permute-start.64 = (f32[128,128]{1,0:T(8,128)S(1)}, f32[128,128]{1,0:T(8,128)S(1)}, u32[]{:S(2)}, u32[]{:S(2)}) collective-permute-start(f32[128,128]{1,0:T(8,128)S(1)} %get-tuple-element.42.up), channel_id=1, source_target_pairs={{0,1},{1,2},{2,3},{3,4},{4,5},{5,6},{6,7},{8,9},{9,10},{10,11},{11... | collective-permute-start | bytes 196616 | tf_op jit(solution)/shard_map/ppermute | solution.py:372
  7.4 0.7 copy-start.4
  8.2 14.1 %collective-permute-start.7 = (f32[128,128]{1,0:T(8,128)S(1)}, f32[128,128]{1,0:T(8,128)}, u32[]{:S(2)}, u32[]{:S(2)}) collective-permute-start(f32[128,128]{1,0:T(8,128)S(1)} %param.3), channel_id=1, source_target_pairs={{39,7},{23,15},{15,23},{7,31},{255,39},{247,47},{239,55},{231,63},... | collective-permute-start | bytes 196616 | tf_op jit(solution)/shard_map/cond/branch_3_fun/ppermute | solution.py:383
  17.0 7.0 %collective-permute-start.6 = (f32[128,128]{1,0:T(8,128)S(1)}, f32[128,128]{1,0:T(8,128)}, u32[]{:S(2)}, u32[]{:S(2)}) collective-permute-start(f32[128,128]{1,0:T(8,128)S(1)} %param.3), channel_id=1, source_target_pairs={{31,7},{15,15},{7,23},{255,31},{247,39},{239,47},{231,55},{223,63}... | collective-permute-start | bytes 196616 | tf_op jit(solution)/shard_map/cond/branch_3_fun/ppermute | solution.py:383
  24.1 0.6 copy-start
  24.1 0.6 copy-start.1
  26.5 53.1 %collective-permute-start.67 = (f32[288,128]{1,0:T(8,128)}, f32[288,128]{1,0:T(8,128)S(1)}, u32[]{:S(2)}, u32[]{:S(2)}) collective-permute-start(f32[288,128]{1,0:T(8,128)} %get-tuple-element.48), channel_id=1, source_target_pairs={{8,0},{16,8},{24,16},{32,24},{40,32},{48,40},{56,48},{64,56},{72,6... | collective-permute-start | bytes 442376 | tf_op jit(solution)/shard_map/ppermute | solution.py:405
  62.4 17.1 %collective-permute-start.66 = (f32[160,128]{1,0:T(8,128)}, f32[160,128]{1,0:T(8,128)S(1)}, u32[]{:S(2)}, u32[]{:S(2)}) collective-permute-start(f32[160,128]{1,0:T(8,128)} %get-tuple-element.47), channel_id=1, source_target_pairs={{0,8},{8,16},{16,24},{24,32},{32,40},{40,48},{48,56},{56,64},{64,7... | collective-permute-start | bytes 245768 | tf_op jit(solution)/shard_map/ppermute | solution.py:404
  79.5 0.6 copy-start.3
  79.5 0.7 copy-start.2

commit v2 on v1

--- a/solution.py
+++ b/solution.py
@@ -360,10 +360,16 @@
     def like(*shape):
         return jax.ShapeDtypeStruct(shape, F32)
 
+    def on_chip(*shape):
+        return like(*shape) if interpret else pltpu.VMEM(shape, F32)
+
+    def held(x):
+        return x if interpret else pltpu.with_memory_space_constraint(x, pltpu.VMEM)
+
     stack = 4 * rows + 2 * depth
     up, down, cols = call(
         pack_kernel,
-        out_shape=(like(stack, width), like(stack, width), like(16, width)),
+        out_shape=(on_chip(stack, width), on_chip(stack, width), on_chip(16, width)),
         in_specs=[vmem] * 6,
         out_specs=(vmem,) * 3,
         name="pack",
@@ -396,11 +402,11 @@
     edge_rows = 4 * 3 * rows * EDGE // width + 8
     eastward, westward = call(
         edge_kernel,
-        out_shape=(like(edge_rows + stack, width), like(edge_rows + 2 * stack, width)),
+        out_shape=(on_chip(edge_rows + stack, width), on_chip(edge_rows + 2 * stack, width)),
         in_specs=[smem] + [vmem] * 6,
         out_specs=(vmem,) * 2,
         name="edge",
-    )(lon, up, south, north, cols, main, extra)
+    )(lon, *map(held, (up, south, north, cols, main, extra)))
     from_west = lax.ppermute(eastward, "lon", [(i, (i + 1) % n_lon) for i in range(n_lon)])
     from_east = lax.ppermute(westward, "lon", [((i + 1) % n_lon, i) for i in range(n_lon)])
 
@@ -419,8 +425,8 @@
         ],
         name="final",
     )(
-        lon, turn, at_top, horiz_mixing, vert_mixing, tracer, velocity, up, down, south, north, cols,
-        from_west, from_east, main, extra,
+        lon, turn, at_top, horiz_mixing, vert_mixing, tracer, velocity,
+        *map(held, (up, down, south, north, cols, from_west, from_east, main, extra)),
     )
 
 

time: 85.9 us -> 82.9 us (0.965)
  Pallas kernels: 9.3 us -> 7.84 us
  local copies, waits for them, and re-layouts: 1.96 us -> 0.65 us
    pallas_call x2, Pallas kernels: 3.98 us -> 2.63 us  [the longest x1 1.64 us: shards(): call(pack_kernel, out_shape=(on_chip(stack, width), on_chip(stack, width)...]
    unnamed x10 -> x2, local copies, waits for them, and re-layouts: 1.96 us -> 0.65 us
where the time goes in v2:
time: 82.9 us; the launch traced here: 82.6 us
  starting transfers between devices  52 us (63%)
  waiting for transfers between devices  20.6 us (25%)
  Pallas kernels  7.84 us (9%)
  between operations  1.45 us (2%)
    ppermute x1, starting transfers between devices, shards(): lax.ppermute(westward, 'lon', [((i + 1) % n_lon, i) for i in range(n_lon)])  35.4 us
    ppermute x1, waiting for transfers between devices, shards(): lax.ppermute(eastward, 'lon', [(i, (i + 1) % n_lon) for i in range(n_lon)])  14.9 us
    ppermute x2, starting transfers between devices, fetch(): return lax.ppermute(x, ('lon', 'lat'), pairs)  10.8 us
    ppermute x2, waiting for transfers between devices, fetch(): return lax.ppermute(x, ('lon', 'lat'), pairs)  5.68 us
    pallas_call x1, Pallas kernels, shards(): call(functools.partial(final_kernel, n_lon), out_shape=(like(depth, rows,...  5.21 us
    ppermute x1, starting transfers between devices, shards(): north = lax.ppermute(down, 'lat', [(i + 1, i) for i in range(n_lat - 1)])  2.55 us
    ppermute x1, starting transfers between devices, shards(): lax.ppermute(eastward, 'lon', [(i, (i + 1) % n_lon) for i in range(n_lon)])  1.95 us
  transfers between devices with their start and end apart: 6, of which 3 were waited for; matrix products, arithmetic and copies ran while one was open for 0% of the time, Pallas kernels for 0%

profile of v2, /device:TPU:39, one launch (start us, length us, event | category | flops | bytes accessed | tf_op | source)
XLA Modules:
  0.0 82.6 jit_solution(15893734288879960644)
XLA Ops:
  1.3 1.6 %pack.1 = (f32[128,128]{1,0:T(8,128)S(1)}, f32[128,128]{1,0:T(8,128)S(1)}, f32[16,128]{1,0:T(8,128)S(1)}) custom-call(s32[1,1]{1,0:T(1,128)S(6)} %copy.76.land, f32[32,16,128]{2,1,0:T(8,128)} %tracer.3, f32[2,32,16,128]{3,2,1,0:T(8,128)} %velocity.3, f32[16,128]{1,0:T(8,128)} %surface.1, f32[2,16,128]{2,1,0:T(8,128)} %transport.1, s32[16,128]{1,0:T(8,128)} %levels.1), custom_call_target="tpu_custom_call" | custom-call | tf_op jit(solution)/shard_map/pack/pallas_call | solution.py:370
  2.9 2.5 %collective-permute-start.65 = (f32[128,128]{1,0:T(8,128)S(1)}, f32[128,128]{1,0:T(8,128)S(1)}, u32[]{:S(2)}, u32[]{:S(2)}) collective-permute-start(f32[128,128]{1,0:T(8,128)S(1)} %get-tuple-element.43.down), channel_id=1, source_target_pairs={{1,0},{2,1},{3,2},{4,3},{5,4},{6,5},{7,6},{9,8},{10,9},{11,10},{12... | collective-permute-start | bytes 196616 | tf_op jit(solution)/shard_map/ppermute | solution.py:379
  5.5 1.3 %collective-permute-start.64 = (f32[128,128]{1,0:T(8,128)S(1)}, f32[128,128]{1,0:T(8,128)S(1)}, u32[]{:S(2)}, u32[]{:S(2)}) collective-permute-start(f32[128,128]{1,0:T(8,128)S(1)} %get-tuple-element.42.up), channel_id=1, source_target_pairs={{0,1},{1,2},{2,3},{3,4},{4,5},{5,6},{6,7},{8,9},{9,10},{10,11},{11... | collective-permute-start | bytes 196616 | tf_op jit(solution)/shard_map/ppermute | solution.py:378
  6.8 0.0 copy-start
  6.8 0.6 copy-done
  7.6 16.5 %conditional.1 = (f32[128,128]{1,0:T(8,128)}, f32[128,128]{1,0:T(8,128)}) conditional(s32[]{:T(128)} %clamp.3, f32[128,128]{1,0:T(8,128)S(1)} %get-tuple-element.42.up, f32[128,128]{1,0:T(8,128)S(1)} %get-tuple-element.42.up, f32[128,128]{1,0:T(8,128)S(1)} %get-tuple-element.42.up, ...), branch_computations={%region_0.1_spmd, %region_1.2_spmd, %region_2.3_spmd, %region_3.4_... | conditional | bytes 524384 | solution.py:398
  7.6 8.9 %collective-permute-start.7 = (f32[128,128]{1,0:T(8,128)S(1)}, f32[128,128]{1,0:T(8,128)}, u32[]{:S(2)}, u32[]{:S(2)}) collective-permute-start(f32[128,128]{1,0:T(8,128)S(1)} %param.3), channel_id=1, source_target_pairs={{39,7},{23,15},{15,23},{7,31},{255,39},{247,47},{239,55},{231,63},... | collective-permute-start | bytes 196616 | tf_op jit(solution)/shard_map/cond/branch_3_fun/ppermute | solution.py:389
  16.5 2.0 %collective-permute-start.6 = (f32[128,128]{1,0:T(8,128)S(1)}, f32[128,128]{1,0:T(8,128)}, u32[]{:S(2)}, u32[]{:S(2)}) collective-permute-start(f32[128,128]{1,0:T(8,128)S(1)} %param.3), channel_id=1, source_target_pairs={{31,7},{15,15},{7,23},{255,31},{247,39},{239,47},{231,55},{223,63}... | collective-permute-start | bytes 196616 | tf_op jit(solution)/shard_map/cond/branch_3_fun/ppermute | solution.py:389
  18.4 3.3 %collective-permute-done.7 = f32[128,128]{1,0:T(8,128)} collective-permute-done((f32[128,128]{1,0:T(8,128)S(1)}, f32[128,128]{1,0:T(8,128)}, u32[]{:S(2)}, u32[]{:S(2)}) %collective-permute-start.7) | collective-permute-done | bytes 65568 | tf_op jit(solution)/shard_map/cond/branch_3_fun/ppermute | solution.py:389
  21.7 2.4 %collective-permute-done.6 = f32[128,128]{1,0:T(8,128)} collective-permute-done((f32[128,128]{1,0:T(8,128)S(1)}, f32[128,128]{1,0:T(8,128)}, u32[]{:S(2)}, u32[]{:S(2)}) %collective-permute-start.6) | collective-permute-done | bytes 65568 | tf_op jit(solution)/shard_map/cond/branch_3_fun/ppermute | solution.py:389
  24.1 0.0 collective-permute-done.65.north
  24.1 0.0 collective-permute-done.64.south
  24.1 1.0 %edge.1 = (f32[160,128]{1,0:T(8,128)S(1)}, f32[288,128]{1,0:T(8,128)S(1)}) custom-call(s32[1]{0:T(128)} %bitcast.lon.lon_ref, f32[128,128]{1,0:T(8,128)S(1)} %get-tuple-element.42.up, f32[128,128]{1,0:T(8,128)S(1)} %collective-permute-done.64.south, f32[128,128]{1,0:T(8,128)S(1)} %collective-permute-done.65.north, f32[16,128]{1,0:T(8,128)S(1)} %get-tuple-element.44.cols, ...), custom_call_target="tpu_custom_call" | custom-call | tf_op jit(solution)/shard_map/edge/pallas_call | solution.py:403
  25.1 35.4 %collective-permute-start.67 = (f32[288,128]{1,0:T(8,128)S(1)}, f32[288,128]{1,0:T(8,128)S(1)}, u32[]{:S(2)}, u32[]{:S(2)}) collective-permute-start(f32[288,128]{1,0:T(8,128)S(1)} %get-tuple-element.48), channel_id=1, source_target_pairs={{8,0},{16,8},{24,16},{32,24},{40,32},{48,40},{56,48},{64,56},{72,6... | collective-permute-start | bytes 442376 | tf_op jit(solution)/shard_map/ppermute | solution.py:411
  60.5 2.0 %collective-permute-start.66 = (f32[160,128]{1,0:T(8,128)S(1)}, f32[160,128]{1,0:T(8,128)S(1)}, u32[]{:S(2)}, u32[]{:S(2)}) collective-permute-start(f32[160,128]{1,0:T(8,128)S(1)} %get-tuple-element.47), channel_id=1, source_target_pairs={{0,8},{8,16},{16,24},{24,32},{32,40},{40,48},{48,56},{56,64},{64,7... | collective-permute-start | bytes 245768 | tf_op jit(solution)/shard_map/ppermute | solution.py:410
  62.4 14.9 %collective-permute-done.66.from_west = f32[160,128]{1,0:T(8,128)S(1)} collective-permute-done((f32[160,128]{1,0:T(8,128)S(1)}, f32[160,128]{1,0:T(8,128)S(1)}, u32[]{:S(2)}, u32[]{:S(2)}) %collective-permute-start.66) | collective-permute-done | bytes 81952 | tf_op jit(solution)/shard_map/ppermute | solution.py:410
  77.4 0.0 collective-permute-done.67.from_east
  77.4 5.2 %final.1 = (f32[32,16,128]{2,1,0:T(8,128)}, f32[16,128]{1,0:T(8,128)}, f32[2,16,128]{2,1,0:T(8,128)}) custom-call(s32[1]{0:T(128)} %bitcast.lon.lon_ref, s32[1]{0:T(128)} %bitcast.2.turn_ref, s32[1]{0:T(128)} %bitcast.3.top_ref, f32[32]{0:T(128)} %hmix.1, f32[31]{0:T(128)} %vmix.1, f32[32,16,128]{2,1,0:T(8,128)} %tracer.3, f32[2,32,16,128]{3,2,1,0:T(8,128)} %velocity.3, ...), custom_call_target="tpu_custom_call" | custom-call | tf_op jit(solution)/shard_map/final/pallas_call | solution.py:413
Async XLA Ops:
  2.9 21.2 %collective-permute-start.65 = (f32[128,128]{1,0:T(8,128)S(1)}, f32[128,128]{1,0:T(8,128)S(1)}, u32[]{:S(2)}, u32[]{:S(2)}) collective-permute-start(f32[128,128]{1,0:T(8,128)S(1)} %get-tuple-element.43.down), channel_id=1, source_target_pairs={{1,0},{2,1},{3,2},{4,3},{5,4},{6,5},{7,6},{9,8},{10,9},{11,10},{12... | collective-permute-start | bytes 196616 | tf_op jit(solution)/shard_map/ppermute | solution.py:379
  5.5 18.6 %collective-permute-start.64 = (f32[128,128]{1,0:T(8,128)S(1)}, f32[128,128]{1,0:T(8,128)S(1)}, u32[]{:S(2)}, u32[]{:S(2)}) collective-permute-start(f32[128,128]{1,0:T(8,128)S(1)} %get-tuple-element.42.up), channel_id=1, source_target_pairs={{0,1},{1,2},{2,3},{3,4},{4,5},{5,6},{6,7},{8,9},{9,10},{10,11},{11... | collective-permute-start | bytes 196616 | tf_op jit(solution)/shard_map/ppermute | solution.py:378
  6.8 0.7 copy-start
  7.6 14.1 %collective-permute-start.7 = (f32[128,128]{1,0:T(8,128)S(1)}, f32[128,128]{1,0:T(8,128)}, u32[]{:S(2)}, u32[]{:S(2)}) collective-permute-start(f32[128,128]{1,0:T(8,128)S(1)} %param.3), channel_id=1, source_target_pairs={{39,7},{23,15},{15,23},{7,31},{255,39},{247,47},{239,55},{231,63},... | collective-permute-start | bytes 196616 | tf_op jit(solution)/shard_map/cond/branch_3_fun/ppermute | solution.py:389
  16.5 7.6 %collective-permute-start.6 = (f32[128,128]{1,0:T(8,128)S(1)}, f32[128,128]{1,0:T(8,128)}, u32[]{:S(2)}, u32[]{:S(2)}) collective-permute-start(f32[128,128]{1,0:T(8,128)S(1)} %param.3), channel_id=1, source_target_pairs={{31,7},{15,15},{7,23},{255,31},{247,39},{239,47},{231,55},{223,63}... | collective-permute-start | bytes 196616 | tf_op jit(solution)/shard_map/cond/branch_3_fun/ppermute | solution.py:389
  25.1 52.3 %collective-permute-start.67 = (f32[288,128]{1,0:T(8,128)S(1)}, f32[288,128]{1,0:T(8,128)S(1)}, u32[]{:S(2)}, u32[]{:S(2)}) collective-permute-start(f32[288,128]{1,0:T(8,128)S(1)} %get-tuple-element.48), channel_id=1, source_target_pairs={{8,0},{16,8},{24,16},{32,24},{40,32},{48,40},{56,48},{64,56},{72,6... | collective-permute-start | bytes 442376 | tf_op jit(solution)/shard_map/ppermute | solution.py:411
  60.5 16.9 %collective-permute-start.66 = (f32[160,128]{1,0:T(8,128)S(1)}, f32[160,128]{1,0:T(8,128)S(1)}, u32[]{:S(2)}, u32[]{:S(2)}) collective-permute-start(f32[160,128]{1,0:T(8,128)S(1)} %get-tuple-element.47), channel_id=1, source_target_pairs={{0,8},{8,16},{16,24},{24,32},{32,40},{40,48},{48,56},{56,64},{64,7... | collective-permute-start | bytes 245768 | tf_op jit(solution)/shard_map/ppermute | solution.py:410

commit v3 on v2

--- a/solution.py
+++ b/solution.py
@@ -88,12 +88,58 @@
     westward[at + size : at + 2 * size] = extra[...]
 
 
+def face(near, beyond, wet_near, wet_beyond, vel_near, vel_beyond, mixing):
+    flux = mixing * (beyond - near) - 0.25 * (vel_near + vel_beyond) * (near + beyond)
+    return jnp.where(jnp.logical_and(wet_near, wet_beyond), flux, 0.0)
+
+
+def interior_kernel(hmix, vmix, tracer, velocity, up, inner, inverses, carries, primes):
+    depth, rows, width = tracer.shape
+    here = up[3 * rows : 4 * rows]
+    lane = lanes_of((rows, width))
+    row = rows_of((rows, width))
+    here_east = roll(here, -1, 1)
+    here_north = roll(here, -1, 0)
+    prime = link = None
+    for k in range(depth):
+        field, zonal, merid = tracer[k], velocity[0, k], velocity[1, k]
+        wet = here > k
+        mixing = hmix[k]
+        east_flux = face(
+            field, roll(field, -1, 1), wet, here_east > k, zonal, roll(zonal, -1, 1), mixing
+        )
+        east_flux = jnp.where(lane == width - 1, 0.0, east_flux)
+        north_flux = face(
+            field, roll(field, -1, 0), wet, here_north > k, merid, roll(merid, -1, 0), mixing
+        )
+        north_flux = jnp.where(row == rows - 1, 0.0, north_flux)
+        inner[k] = field + (
+            (east_flux - roll(east_flux, 1, 1)) + (north_flux - roll(north_flux, 1, 0))
+        )
+        diagonal = jnp.ones_like(field)
+        if k > 0:
+            diagonal = diagonal + link
+        if k < depth - 1:
+            next_link = jnp.where(here > k + 1, vmix[k], 0.0)
+            diagonal = diagonal + next_link
+        if k > 0:
+            diagonal = diagonal + link * prime
+        inverse = 1.0 / diagonal
+        inverses[k] = inverse
+        if k > 0:
+            carries[k - 1] = link * inverse
+        if k < depth - 1:
+            prime = -next_link * inverse
+            primes[k] = prime
+            link = next_link
+
+
 def final_kernel(
-    n_lon, lon_ref, turn_ref, top_ref, hmix, vmix, tracer, velocity, up, down, south, north, cols, from_west, from_east, main, extra,
+    n_lon, lon_ref, turn_ref, top_ref, hmix, inner, inverses, carries, primes, up, down, south, north, cols, from_west, from_east, main, extra,
     tracer_out, surface_out, transport_out,
-    north_own, north_far, seam_own, seam_far, north_rows, primes,
+    north_own, north_far, seam_own, seam_far, north_rows,
 ):
-    depth, rows, width = tracer.shape
+    depth, rows, width = inner.shape
     groups = width // EDGE
     lane8 = lanes_of((8, width))
     half_way = width // 2
@@ -238,10 +284,6 @@
     transport_out[0] = u[mid]
     transport_out[1] = v[mid]
 
-    def face(near, beyond, wet_near, wet_beyond, vel_near, vel_beyond, mixing):
-        flux = mixing * (beyond - near) - 0.25 * (vel_near + vel_beyond) * (near + beyond)
-        return jnp.where(jnp.logical_and(wet_near, wet_beyond), flux, 0.0)
-
     level_row = rows_of((depth, width)).astype(F32)
     mix_rows = jnp.zeros((depth, width), F32)
     for k in range(depth):
@@ -299,8 +341,6 @@
 
     lane = lanes_of((rows, width))
     row = rows_of((rows, width))
-    here_east = roll(here, -1, 1)
-    here_north = roll(here, -1, 0)
 
     def spread(x, k):
         return jnp.concatenate(
@@ -308,40 +348,16 @@
             axis=0,
         )
 
-    sweep = prime = link = None
+    sweep = None
     for k in range(depth):
-        field, zonal, merid = tracer[k], velocity[0, k], velocity[1, k]
-        wet = here > k
-        mixing = hmix[k]
-        east_flux = face(
-            field, roll(field, -1, 1), wet, here_east > k, zonal, roll(zonal, -1, 1), mixing
-        )
-        east_flux = jnp.where(lane == width - 1, spread(flux_right, k), east_flux)
-        west_flux = jnp.where(lane == 0, spread(flux_left, k), roll(east_flux, 1, 1))
-        north_flux = face(
-            field, roll(field, -1, 0), wet, here_north > k, merid, roll(merid, -1, 0), mixing
-        )
-        north_flux = jnp.where(row == rows - 1, flux_top[k : k + 1], north_flux)
-        south_flux = jnp.where(row == 0, flux_bottom[k : k + 1], roll(north_flux, 1, 0))
-        stepped = jnp.where(
-            wet, field + ((east_flux - west_flux) + (north_flux - south_flux)), 0.0
-        )
-        diagonal = jnp.ones_like(stepped)
-        if k > 0:
-            diagonal = diagonal + link
-        if k < depth - 1:
-            next_link = jnp.where(here > k + 1, vmix[k], 0.0)
-            diagonal = diagonal + next_link
-        if k > 0:
-            diagonal = diagonal + link * prime
-            stepped = stepped + link * sweep
-        inverse = 1.0 / diagonal
-        sweep = stepped * inverse
+        lateral = jnp.where(lane == width - 1, spread(flux_right, k), 0.0)
+        lateral = lateral - jnp.where(lane == 0, spread(flux_left, k), 0.0)
+        lateral = lateral + jnp.where(row == rows - 1, flux_top[k : k + 1], 0.0)
+        lateral = lateral - jnp.where(row == 0, flux_bottom[k : k + 1], 0.0)
+        stepped = jnp.where(here > k, inner[k] + lateral, 0.0)
+        reduced = stepped * inverses[k]
+        sweep = reduced if k == 0 else reduced + carries[k - 1] * sweep
         tracer_out[k] = sweep
-        if k < depth - 1:
-            prime = -next_link * inverse
-            primes[k] = prime
-            link = next_link
     solved = sweep
     for k in range(depth - 2, -1, -1):
         solved = tracer_out[k] - primes[k] * solved
@@ -410,10 +426,22 @@
     from_west = lax.ppermute(eastward, "lon", [(i, (i + 1) % n_lon) for i in range(n_lon)])
     from_east = lax.ppermute(westward, "lon", [((i + 1) % n_lon, i) for i in range(n_lon)])
 
+    inner, inverses, carries, primes = call(
+        interior_kernel,
+        out_shape=(
+            on_chip(depth, rows, width),
+            on_chip(depth, rows, width),
+            on_chip(depth - 1, rows, width),
+            on_chip(depth - 1, rows, width),
+        ),
+        in_specs=[smem] * 2 + [vmem] * 3,
+        out_specs=(vmem,) * 4,
+        name="interior",
+    )(horiz_mixing, vert_mixing, tracer, velocity, held(up))
     return call(
         functools.partial(final_kernel, n_lon),
         out_shape=(like(depth, rows, width), like(rows, width), like(2, rows, width)),
-        in_specs=[smem] * 5 + [vmem] * 11,
+        in_specs=[smem] * 4 + [vmem] * 13,
         out_specs=(vmem,) * 3,
         scratch_shapes=[
             pltpu.VMEM((4 * rows, width), F32),
@@ -421,11 +449,10 @@
             pltpu.VMEM((8, width), F32),
             pltpu.VMEM((8, width), F32),
             pltpu.VMEM((2 * depth, width), F32),
-            pltpu.VMEM((depth, rows, width), F32),
         ],
         name="final",
     )(
-        lon, turn, at_top, horiz_mixing, vert_mixing, tracer, velocity,
+        lon, turn, at_top, horiz_mixing, *map(held, (inner, inverses, carries, primes)),
         *map(held, (up, down, south, north, cols, from_west, from_east, main, extra)),
     )
 

time: 82.9 us -> 81.8 us (0.987)
  waiting for transfers between devices: 20.6 us -> 18.5 us
  Pallas kernels: 7.84 us -> 8.8 us
    ppermute x1, waiting for transfers between devices: 14.9 us -> 12.8 us  [shards(): lax.ppermute(eastward, 'lon', [(i, (i + 1) % n_lon) for i in range(n_lon)])]
    pallas_call x0 -> x1, Pallas kernels: none -> 2.09 us  [shards(): call(interior_kernel, out_shape=(on_chip(depth, rows, width), on_chip(dep...]
    pallas_call x1, Pallas kernels: 5.21 us -> 4.08 us  [shards(): call(functools.partial(final_kernel, n_lon), out_shape=(like(depth, rows,...]
  transfers between devices with their start and end apart: 6 -> 6, of which waited for: 3 -> 3; matrix products, arithmetic and copies ran while one was open for 0% -> 0% of each run, Pallas kernels for 0% -> 3%
where the time goes in v3:
time: 81.8 us; the launch traced here: 81.5 us
  starting transfers between devices  52 us (64%)
  waiting for transfers between devices  18.5 us (23%)
  Pallas kernels  8.8 us (11%)
  between operations  1.46 us (2%)
    ppermute x1, starting transfers between devices, shards(): lax.ppermute(westward, 'lon', [((i + 1) % n_lon, i) for i in range(n_lon)])  35.4 us
    ppermute x1, waiting for transfers between devices, shards(): lax.ppermute(eastward, 'lon', [(i, (i + 1) % n_lon) for i in range(n_lon)])  12.8 us
    ppermute x2, starting transfers between devices, fetch(): return lax.ppermute(x, ('lon', 'lat'), pairs)  10.8 us
    ppermute x2, waiting for transfers between devices, fetch(): return lax.ppermute(x, ('lon', 'lat'), pairs)  5.68 us
    pallas_call x1, Pallas kernels, shards(): call(functools.partial(final_kernel, n_lon), out_shape=(like(depth, rows,...  4.08 us
    ppermute x1, starting transfers between devices, shards(): north = lax.ppermute(down, 'lat', [(i + 1, i) for i in range(n_lat - 1)])  2.55 us
    pallas_call x1, Pallas kernels, shards(): call(interior_kernel, out_shape=(on_chip(depth, rows, width), on_chip(dep...  2.09 us
    ppermute x1, starting transfers between devices, shards(): lax.ppermute(eastward, 'lon', [(i, (i + 1) % n_lon) for i in range(n_lon)])  1.95 us
  transfers between devices with their start and end apart: 6, of which 3 were waited for; matrix products, arithmetic and copies ran while one was open for 0% of the time, Pallas kernels for 3%

profile of v3, /device:TPU:39, one launch (start us, length us, event | category | flops | bytes accessed | tf_op | source)
XLA Modules:
  0.0 81.5 jit_solution(17400317596294129119)
XLA Ops:
  1.3 1.6 %pack.1 = (f32[128,128]{1,0:T(8,128)S(1)}, f32[128,128]{1,0:T(8,128)S(1)}, f32[16,128]{1,0:T(8,128)S(1)}) custom-call(s32[1,1]{1,0:T(1,128)S(6)} %copy.76.land, f32[32,16,128]{2,1,0:T(8,128)} %tracer.3, f32[2,32,16,128]{3,2,1,0:T(8,128)} %velocity.3, f32[16,128]{1,0:T(8,128)} %surface.1, f32[2,16,128]{2,1,0:T(8,128)} %transport.1, s32[16,128]{1,0:T(8,128)} %levels.1), custom_call_target="tpu_custom_call" | custom-call | tf_op jit(solution)/shard_map/pack/pallas_call | solution.py:386
  2.9 2.5 %collective-permute-start.65 = (f32[128,128]{1,0:T(8,128)S(1)}, f32[128,128]{1,0:T(8,128)S(1)}, u32[]{:S(2)}, u32[]{:S(2)}) collective-permute-start(f32[128,128]{1,0:T(8,128)S(1)} %get-tuple-element.51.down), channel_id=1, source_target_pairs={{1,0},{2,1},{3,2},{4,3},{5,4},{6,5},{7,6},{9,8},{10,9},{11,10},{12... | collective-permute-start | bytes 196616 | tf_op jit(solution)/shard_map/ppermute | solution.py:395
  5.5 1.3 %collective-permute-start.64 = (f32[128,128]{1,0:T(8,128)S(1)}, f32[128,128]{1,0:T(8,128)S(1)}, u32[]{:S(2)}, u32[]{:S(2)}) collective-permute-start(f32[128,128]{1,0:T(8,128)S(1)} %get-tuple-element.46.up), channel_id=1, source_target_pairs={{0,1},{1,2},{2,3},{3,4},{4,5},{5,6},{6,7},{8,9},{9,10},{10,11},{11... | collective-permute-start | bytes 196616 | tf_op jit(solution)/shard_map/ppermute | solution.py:394
  6.8 0.0 copy-start
  6.8 0.6 copy-done
  7.6 16.5 %conditional.1 = (f32[128,128]{1,0:T(8,128)}, f32[128,128]{1,0:T(8,128)}) conditional(s32[]{:T(128)} %clamp.3, f32[128,128]{1,0:T(8,128)S(1)} %get-tuple-element.46.up, f32[128,128]{1,0:T(8,128)S(1)} %get-tuple-element.46.up, f32[128,128]{1,0:T(8,128)S(1)} %get-tuple-element.46.up, ...), branch_computations={%region_0.1_spmd, %region_1.2_spmd, %region_2.3_spmd, %region_3.4_... | conditional | bytes 524384 | solution.py:414
  7.6 8.9 %collective-permute-start.7 = (f32[128,128]{1,0:T(8,128)S(1)}, f32[128,128]{1,0:T(8,128)}, u32[]{:S(2)}, u32[]{:S(2)}) collective-permute-start(f32[128,128]{1,0:T(8,128)S(1)} %param.3), channel_id=1, source_target_pairs={{39,7},{23,15},{15,23},{7,31},{255,39},{247,47},{239,55},{231,63},... | collective-permute-start | bytes 196616 | tf_op jit(solution)/shard_map/cond/branch_3_fun/ppermute | solution.py:405
  16.5 2.0 %collective-permute-start.6 = (f32[128,128]{1,0:T(8,128)S(1)}, f32[128,128]{1,0:T(8,128)}, u32[]{:S(2)}, u32[]{:S(2)}) collective-permute-start(f32[128,128]{1,0:T(8,128)S(1)} %param.3), channel_id=1, source_target_pairs={{31,7},{15,15},{7,23},{255,31},{247,39},{239,47},{231,55},{223,63}... | collective-permute-start | bytes 196616 | tf_op jit(solution)/shard_map/cond/branch_3_fun/ppermute | solution.py:405
  18.4 3.3 %collective-permute-done.7 = f32[128,128]{1,0:T(8,128)} collective-permute-done((f32[128,128]{1,0:T(8,128)S(1)}, f32[128,128]{1,0:T(8,128)}, u32[]{:S(2)}, u32[]{:S(2)}) %collective-permute-start.7) | collective-permute-done | bytes 65568 | tf_op jit(solution)/shard_map/cond/branch_3_fun/ppermute | solution.py:405
  21.7 2.4 %collective-permute-done.6 = f32[128,128]{1,0:T(8,128)} collective-permute-done((f32[128,128]{1,0:T(8,128)S(1)}, f32[128,128]{1,0:T(8,128)}, u32[]{:S(2)}, u32[]{:S(2)}) %collective-permute-start.6) | collective-permute-done | bytes 65568 | tf_op jit(solution)/shard_map/cond/branch_3_fun/ppermute | solution.py:405
  24.1 0.0 collective-permute-done.65.north
  24.1 0.0 collective-permute-done.64.south
  24.1 1.0 %edge.1 = (f32[160,128]{1,0:T(8,128)S(1)}, f32[288,128]{1,0:T(8,128)S(1)}) custom-call(s32[1]{0:T(128)} %bitcast.lon.lon_ref, f32[128,128]{1,0:T(8,128)S(1)} %get-tuple-element.46.up, f32[128,128]{1,0:T(8,128)S(1)} %collective-permute-done.64.south, f32[128,128]{1,0:T(8,128)S(1)} %collective-permute-done.65.north, f32[16,128]{1,0:T(8,128)S(1)} %get-tuple-element.52.cols, ...), custom_call_target="tpu_custom_call" | custom-call | tf_op jit(solution)/shard_map/edge/pallas_call | solution.py:419
  25.1 35.4 %collective-permute-start.67 = (f32[288,128]{1,0:T(8,128)S(1)}, f32[288,128]{1,0:T(8,128)S(1)}, u32[]{:S(2)}, u32[]{:S(2)}) collective-permute-start(f32[288,128]{1,0:T(8,128)S(1)} %get-tuple-element.56), channel_id=1, source_target_pairs={{8,0},{16,8},{24,16},{32,24},{40,32},{48,40},{56,48},{64,56},{72,6... | collective-permute-start | bytes 442376 | tf_op jit(solution)/shard_map/ppermute | solution.py:427
  60.5 2.0 %collective-permute-start.66 = (f32[160,128]{1,0:T(8,128)S(1)}, f32[160,128]{1,0:T(8,128)S(1)}, u32[]{:S(2)}, u32[]{:S(2)}) collective-permute-start(f32[160,128]{1,0:T(8,128)S(1)} %get-tuple-element.55), channel_id=1, source_target_pairs={{0,8},{8,16},{16,24},{24,32},{32,40},{40,48},{48,56},{56,64},{64,7... | collective-permute-start | bytes 245768 | tf_op jit(solution)/shard_map/ppermute | solution.py:426
  62.4 2.1 %interior.1 = (f32[32,16,128]{2,1,0:T(8,128)S(1)}, f32[32,16,128]{2,1,0:T(8,128)S(1)}, f32[31,16,128]{2,1,0:T(8,128)S(1)}, f32[31,16,128]{2,1,0:T(8,128)S(1)}) custom-call(f32[32]{0:T(128)} %hmix.3, f32[31]{0:T(128)} %vmix.1, f32[32,16,128]{2,1,0:T(8,128)} %tracer.3, f32[2,32,16,128]{3,2,1,0:T(8,128)} %velocity.3, f32[128,128]{1,0:T(8,128)S(1)} %get-tuple-element.46.up), custom_call_target="tpu_custom_call" | custom-call | tf_op jit(solution)/shard_map/interior/pallas_call | solution.py:429
  64.5 12.8 %collective-permute-done.66.from_west = f32[160,128]{1,0:T(8,128)S(1)} collective-permute-done((f32[160,128]{1,0:T(8,128)S(1)}, f32[160,128]{1,0:T(8,128)S(1)}, u32[]{:S(2)}, u32[]{:S(2)}) %collective-permute-start.66) | collective-permute-done | bytes 81952 | tf_op jit(solution)/shard_map/ppermute | solution.py:426
  77.4 0.0 collective-permute-done.67.from_east
  77.4 4.1 %final.1 = (f32[32,16,128]{2,1,0:T(8,128)}, f32[16,128]{1,0:T(8,128)}, f32[2,16,128]{2,1,0:T(8,128)}) custom-call(s32[1]{0:T(128)} %bitcast.lon.lon_ref, s32[1]{0:T(128)} %bitcast.2.turn_ref, s32[1]{0:T(128)} %bitcast.3.top_ref, f32[32]{0:T(128)} %hmix.3, f32[32,16,128]{2,1,0:T(8,128)S(1)} %get-tuple-element.47.inner, ...), custom_call_target="tpu_custom_call" | custom-call | tf_op jit(solution)/shard_map/final/pallas_call | solution.py:441
Async XLA Ops:
  2.9 21.2 %collective-permute-start.65 = (f32[128,128]{1,0:T(8,128)S(1)}, f32[128,128]{1,0:T(8,128)S(1)}, u32[]{:S(2)}, u32[]{:S(2)}) collective-permute-start(f32[128,128]{1,0:T(8,128)S(1)} %get-tuple-element.51.down), channel_id=1, source_target_pairs={{1,0},{2,1},{3,2},{4,3},{5,4},{6,5},{7,6},{9,8},{10,9},{11,10},{12... | collective-permute-start | bytes 196616 | tf_op jit(solution)/shard_map/ppermute | solution.py:395
  5.5 18.6 %collective-permute-start.64 = (f32[128,128]{1,0:T(8,128)S(1)}, f32[128,128]{1,0:T(8,128)S(1)}, u32[]{:S(2)}, u32[]{:S(2)}) collective-permute-start(f32[128,128]{1,0:T(8,128)S(1)} %get-tuple-element.46.up), channel_id=1, source_target_pairs={{0,1},{1,2},{2,3},{3,4},{4,5},{5,6},{6,7},{8,9},{9,10},{10,11},{11... | collective-permute-start | bytes 196616 | tf_op jit(solution)/shard_map/ppermute | solution.py:394
  6.8 0.7 copy-start
  7.6 14.1 %collective-permute-start.7 = (f32[128,128]{1,0:T(8,128)S(1)}, f32[128,128]{1,0:T(8,128)}, u32[]{:S(2)}, u32[]{:S(2)}) collective-permute-start(f32[128,128]{1,0:T(8,128)S(1)} %param.3), channel_id=1, source_target_pairs={{39,7},{23,15},{15,23},{7,31},{255,39},{247,47},{239,55},{231,63},... | collective-permute-start | bytes 196616 | tf_op jit(solution)/shard_map/cond/branch_3_fun/ppermute | solution.py:405
  16.5 7.6 %collective-permute-start.6 = (f32[128,128]{1,0:T(8,128)S(1)}, f32[128,128]{1,0:T(8,128)}, u32[]{:S(2)}, u32[]{:S(2)}) collective-permute-start(f32[128,128]{1,0:T(8,128)S(1)} %param.3), channel_id=1, source_target_pairs={{31,7},{15,15},{7,23},{255,31},{247,39},{239,47},{231,55},{223,63}... | collective-permute-start | bytes 196616 | tf_op jit(solution)/shard_map/cond/branch_3_fun/ppermute | solution.py:405
  25.1 52.3 %collective-permute-start.67 = (f32[288,128]{1,0:T(8,128)S(1)}, f32[288,128]{1,0:T(8,128)S(1)}, u32[]{:S(2)}, u32[]{:S(2)}) collective-permute-start(f32[288,128]{1,0:T(8,128)S(1)} %get-tuple-element.56), channel_id=1, source_target_pairs={{8,0},{16,8},{24,16},{32,24},{40,32},{48,40},{56,48},{64,56},{72,6... | collective-permute-start | bytes 442376 | tf_op jit(solution)/shard_map/ppermute | solution.py:427
  60.5 16.9 %collective-permute-start.66 = (f32[160,128]{1,0:T(8,128)S(1)}, f32[160,128]{1,0:T(8,128)S(1)}, u32[]{:S(2)}, u32[]{:S(2)}) collective-permute-start(f32[160,128]{1,0:T(8,128)S(1)} %get-tuple-element.55), channel_id=1, source_target_pairs={{0,8},{8,16},{16,24},{24,32},{32,40},{40,48},{48,56},{56,64},{64,7... | collective-permute-start | bytes 245768 | tf_op jit(solution)/shard_map/ppermute | solution.py:426

commit v4 on v3

--- a/solution.py
+++ b/solution.py
@@ -27,9 +27,16 @@
     return pltpu.roll(x, shift % x.shape[axis], axis)
 
 
-def pack_kernel(land, tracer, velocity, surface, transport, levels, up, down, cols):
+def pack_kernel(
+    n_lon, lon, land, fold_pair, tracer, velocity, surface, transport, levels, up, down, cols, where
+):
     depth, rows, width = tracer.shape
-    real = (levels[...] * (1 - land[...])).astype(F32)
+    pivot = lax.rem(fold_pair[0] + width * lon[0], width * n_lon)
+    turn = lax.rem(pivot, width)
+    behind = jnp.where(turn < width // 2, n_lon - 1, n_lon)
+    where[0] = lax.rem(lax.div(pivot, width) + behind, n_lon)
+    where[1] = turn
+    real = (levels[...] * (1 - land[0, 0])).astype(F32)
     for out, row in ((up, rows - 1), (down, 0)):
         out[0:rows] = surface[...]
         out[rows : 2 * rows] = transport[0]
@@ -174,7 +181,7 @@
 
     @pl.when(at_top)
     def _():
-        turn = turn_ref[0]
+        turn = turn_ref[1]
         small = jnp.full((8, width), turn, jnp.int32) < half_way
         index = (turn - lane8) & (width - 1)
         less = lane8 <= turn
@@ -372,6 +379,7 @@
     smem = pl.BlockSpec(memory_space=pltpu.SMEM)
     vmem = pl.BlockSpec(memory_space=pltpu.VMEM)
     call = functools.partial(pl.pallas_call, interpret=interpret)
+    packed = pltpu.CompilerParams()
 
     def like(*shape):
         return jax.ShapeDtypeStruct(shape, F32)
@@ -383,21 +391,23 @@
         return x if interpret else pltpu.with_memory_space_constraint(x, pltpu.VMEM)
 
     stack = 4 * rows + 2 * depth
-    up, down, cols = call(
-        pack_kernel,
-        out_shape=(on_chip(stack, width), on_chip(stack, width), on_chip(16, width)),
-        in_specs=[vmem] * 6,
-        out_specs=(vmem,) * 3,
+    lon = lax.axis_index("lon")
+    place = lon.reshape(1)
+    up, down, cols, where = call(
+        functools.partial(pack_kernel, n_lon),
+        out_shape=(
+            on_chip(stack, width),
+            on_chip(stack, width),
+            on_chip(16, width),
+            jax.ShapeDtypeStruct((2,), jnp.int32) if interpret else pltpu.SMEM((2,), jnp.int32),
+        ),
+        in_specs=[smem] * 3 + [vmem] * 5,
+        out_specs=(vmem,) * 3 + (smem,),
         name="pack",
-    )(land_tiles, tracer, velocity, surface, transport, levels)
+    )(place, land_tiles, fold_pair, tracer, velocity, surface, transport, levels)
 
     south = lax.ppermute(up, "lat", [(i, i + 1) for i in range(n_lat - 1)])
     north = lax.ppermute(down, "lat", [(i + 1, i) for i in range(n_lat - 1)])
-
-    lon = lax.axis_index("lon")
-    pivot = (fold_pair[0] + width * lon) % (width * n_lon)
-    turn = pivot % width
-    tile = (pivot // width - (turn < width // 2).astype(jnp.int32)) % n_lon
 
     def fetch(x, shift):
         routes = [(shift + 1, 0)] + [(shift - t, t) for t in range(1, n_lon - 1)]
@@ -411,10 +421,10 @@
 
         return both
 
-    extra, main = lax.switch(tile, [branch(shift) for shift in range(n_lon)], up)
+    extra, main = lax.switch(where[0], [branch(shift) for shift in range(n_lon)], up)
 
     at_top = (lax.axis_index("lat") == n_lat - 1).astype(jnp.int32)
-    lon, turn, at_top = (x.reshape(1) for x in (lon, turn, at_top))
+    at_top = at_top.reshape(1)
     edge_rows = 4 * 3 * rows * EDGE // width + 8
     eastward, westward = call(
         edge_kernel,
@@ -422,7 +432,7 @@
         in_specs=[smem] + [vmem] * 6,
         out_specs=(vmem,) * 2,
         name="edge",
-    )(lon, *map(held, (up, south, north, cols, main, extra)))
+    )(place, *map(held, (up, south, north, cols, main, extra)))
     from_west = lax.ppermute(eastward, "lon", [(i, (i + 1) % n_lon) for i in range(n_lon)])
     from_east = lax.ppermute(westward, "lon", [((i + 1) % n_lon, i) for i in range(n_lon)])
 
@@ -436,6 +446,7 @@
         ),
         in_specs=[smem] * 2 + [vmem] * 3,
         out_specs=(vmem,) * 4,
+        compiler_params=packed,
         name="interior",
     )(horiz_mixing, vert_mixing, tracer, velocity, held(up))
     return call(
@@ -450,9 +461,10 @@
             pltpu.VMEM((8, width), F32),
             pltpu.VMEM((2 * depth, width), F32),
         ],
+        compiler_params=packed,
         name="final",
     )(
-        lon, turn, at_top, horiz_mixing, *map(held, (inner, inverses, carries, primes)),
+        place, where, at_top, horiz_mixing, *map(held, (inner, inverses, carries, primes)),
         *map(held, (up, down, south, north, cols, from_west, from_east, main, extra)),
     )
 

time: 81.8 us -> 80.9 us (0.989)
  no operation moved by 1% of the time
where the time goes in v4:
time: 80.9 us; the launch traced here: 80.5 us
  starting transfers between devices  52.4 us (65%)
  waiting for transfers between devices  18.1 us (22%)
  Pallas kernels  8.63 us (11%)
  between operations  1.35 us (2%)
    ppermute x1, starting transfers between devices, shards(): lax.ppermute(westward, 'lon', [((i + 1) % n_lon, i) for i in range(n_lon)])  35.8 us
    ppermute x1, waiting for transfers between devices, shards(): lax.ppermute(eastward, 'lon', [(i, (i + 1) % n_lon) for i in range(n_lon)])  12.8 us
    ppermute x2, starting transfers between devices, fetch(): return lax.ppermute(x, ('lon', 'lat'), pairs)  10.8 us
    ppermute x2, waiting for transfers between devices, fetch(): return lax.ppermute(x, ('lon', 'lat'), pairs)  5.24 us
    pallas_call x1, Pallas kernels, shards(): call(functools.partial(final_kernel, n_lon), out_shape=(like(depth, rows,...  4.08 us
    ppermute x1, starting transfers between devices, shards(): north = lax.ppermute(down, 'lat', [(i + 1, i) for i in range(n_lat - 1)])  2.55 us
    pallas_call x1, Pallas kernels, shards(): call(interior_kernel, out_shape=(on_chip(depth, rows, width), on_chip(dep...  2.09 us
    ppermute x1, starting transfers between devices, shards(): lax.ppermute(eastward, 'lon', [(i, (i + 1) % n_lon) for i in range(n_lon)])  1.95 us
  transfers between devices with their start and end apart: 6, of which 3 were waited for; matrix products, arithmetic and copies ran while one was open for 0% of the time, Pallas kernels for 3%

profile of v4, /device:TPU:39, one launch (start us, length us, event | category | flops | bytes accessed | tf_op | source)
XLA Modules:
  0.0 80.5 jit_solution(969850790293427022)
XLA Ops:
  1.3 1.5 %pack.1 = (f32[128,128]{1,0:T(8,128)S(1)}, f32[128,128]{1,0:T(8,128)S(1)}, f32[16,128]{1,0:T(8,128)S(1)}, s32[2]{0:T(128)S(4)}) custom-call(s32[1]{0:T(128)} %bitcast.lon.lon_ref, s32[1,1]{1,0:T(1,128)S(6)} %copy.76.land, s32[128]{0:T(128)} %fold_pair.1, f32[32,16,128]{2,1,0:T(8,128)} %tracer.3, f32[2,32,16,128]{3,2,1,0:T(8,128)} %velocity.3, ...), custom_call_target="tpu_custom_call" | custom-call | tf_op jit(solution)/shard_map/pack/pallas_call | solution.py:396
  2.8 2.5 %collective-permute-start.65 = (f32[128,128]{1,0:T(8,128)S(1)}, f32[128,128]{1,0:T(8,128)S(1)}, u32[]{:S(2)}, u32[]{:S(2)}) collective-permute-start(f32[128,128]{1,0:T(8,128)S(1)} %get-tuple-element.53.down), channel_id=1, source_target_pairs={{1,0},{2,1},{3,2},{4,3},{5,4},{6,5},{7,6},{9,8},{10,9},{11,10},{12... | collective-permute-start | bytes 196616 | tf_op jit(solution)/shard_map/ppermute | solution.py:410
  5.3 1.3 %collective-permute-start.64 = (f32[128,128]{1,0:T(8,128)S(1)}, f32[128,128]{1,0:T(8,128)S(1)}, u32[]{:S(2)}, u32[]{:S(2)}) collective-permute-start(f32[128,128]{1,0:T(8,128)S(1)} %get-tuple-element.48.up), channel_id=1, source_target_pairs={{0,1},{1,2},{2,3},{3,4},{4,5},{5,6},{6,7},{8,9},{9,10},{10,11},{11... | collective-permute-start | bytes 196616 | tf_op jit(solution)/shard_map/ppermute | solution.py:409
  6.6 16.1 %conditional.1 = (f32[128,128]{1,0:T(8,128)}, f32[128,128]{1,0:T(8,128)}) conditional(s32[]{:T(128)} %bitcast.2, f32[128,128]{1,0:T(8,128)S(1)} %get-tuple-element.48.up, f32[128,128]{1,0:T(8,128)S(1)} %get-tuple-element.48.up, f32[128,128]{1,0:T(8,128)S(1)} %get-tuple-element.48.up, ...), branch_computations={%region_0.0_spmd, %region_1.0_spmd, %region_2.0_spmd, %region_3.0_... | conditional | bytes 524384 | solution.py:424
  6.7 8.9 %collective-permute-start.7 = (f32[128,128]{1,0:T(8,128)S(1)}, f32[128,128]{1,0:T(8,128)}, u32[]{:S(2)}, u32[]{:S(2)}) collective-permute-start(f32[128,128]{1,0:T(8,128)S(1)} %param.3), channel_id=1, source_target_pairs={{39,7},{23,15},{15,23},{7,31},{255,39},{247,47},{239,55},{231,63},... | collective-permute-start | bytes 196616 | tf_op jit(solution)/shard_map/cond/branch_3_fun/ppermute | solution.py:415
  15.5 2.0 %collective-permute-start.6 = (f32[128,128]{1,0:T(8,128)S(1)}, f32[128,128]{1,0:T(8,128)}, u32[]{:S(2)}, u32[]{:S(2)}) collective-permute-start(f32[128,128]{1,0:T(8,128)S(1)} %param.3), channel_id=1, source_target_pairs={{31,7},{15,15},{7,23},{255,31},{247,39},{239,47},{231,55},{223,63}... | collective-permute-start | bytes 196616 | tf_op jit(solution)/shard_map/cond/branch_3_fun/ppermute | solution.py:415
  17.5 3.3 %collective-permute-done.7 = f32[128,128]{1,0:T(8,128)} collective-permute-done((f32[128,128]{1,0:T(8,128)S(1)}, f32[128,128]{1,0:T(8,128)}, u32[]{:S(2)}, u32[]{:S(2)}) %collective-permute-start.7) | collective-permute-done | bytes 65568 | tf_op jit(solution)/shard_map/cond/branch_3_fun/ppermute | solution.py:415
  20.8 2.0 %collective-permute-done.6 = f32[128,128]{1,0:T(8,128)} collective-permute-done((f32[128,128]{1,0:T(8,128)S(1)}, f32[128,128]{1,0:T(8,128)}, u32[]{:S(2)}, u32[]{:S(2)}) %collective-permute-start.6) | collective-permute-done | bytes 65568 | tf_op jit(solution)/shard_map/cond/branch_3_fun/ppermute | solution.py:415
  22.7 0.0 collective-permute-done.65.north
  22.7 0.0 collective-permute-done.64.south
  22.7 1.0 %edge.1 = (f32[160,128]{1,0:T(8,128)S(1)}, f32[288,128]{1,0:T(8,128)S(1)}) custom-call(s32[1]{0:T(128)} %bitcast.lon.lon_ref, f32[128,128]{1,0:T(8,128)S(1)} %get-tuple-element.48.up, f32[128,128]{1,0:T(8,128)S(1)} %collective-permute-done.64.south, f32[128,128]{1,0:T(8,128)S(1)} %collective-permute-done.65.north, f32[16,128]{1,0:T(8,128)S(1)} %get-tuple-element.54.cols, ...), custom_call_target="tpu_custom_call" | custom-call | tf_op jit(solution)/shard_map/edge/pallas_call | solution.py:429
  23.7 35.8 %collective-permute-start.67 = (f32[288,128]{1,0:T(8,128)S(1)}, f32[288,128]{1,0:T(8,128)S(1)}, u32[]{:S(2)}, u32[]{:S(2)}) collective-permute-start(f32[288,128]{1,0:T(8,128)S(1)} %get-tuple-element.58), channel_id=1, source_target_pairs={{8,0},{16,8},{24,16},{32,24},{40,32},{48,40},{56,48},{64,56},{72,6... | collective-permute-start | bytes 442376 | tf_op jit(solution)/shard_map/ppermute | solution.py:437
  59.5 2.0 %collective-permute-start.66 = (f32[160,128]{1,0:T(8,128)S(1)}, f32[160,128]{1,0:T(8,128)S(1)}, u32[]{:S(2)}, u32[]{:S(2)}) collective-permute-start(f32[160,128]{1,0:T(8,128)S(1)} %get-tuple-element.57), channel_id=1, source_target_pairs={{0,8},{8,16},{16,24},{24,32},{32,40},{40,48},{48,56},{56,64},{64,7... | collective-permute-start | bytes 245768 | tf_op jit(solution)/shard_map/ppermute | solution.py:436
  61.5 2.1 %interior.1 = (f32[32,16,128]{2,1,0:T(8,128)S(1)}, f32[32,16,128]{2,1,0:T(8,128)S(1)}, f32[31,16,128]{2,1,0:T(8,128)S(1)}, f32[31,16,128]{2,1,0:T(8,128)S(1)}) custom-call(f32[32]{0:T(128)} %hmix.3, f32[31]{0:T(128)} %vmix.1, f32[32,16,128]{2,1,0:T(8,128)} %tracer.3, f32[2,32,16,128]{3,2,1,0:T(8,128)} %velocity.3, f32[128,128]{1,0:T(8,128)S(1)} %get-tuple-element.48.up), custom_call_target="tpu_custom_call" | custom-call | tf_op jit(solution)/shard_map/interior/pallas_call | solution.py:439
  63.6 12.8 %collective-permute-done.66.from_west = f32[160,128]{1,0:T(8,128)S(1)} collective-permute-done((f32[160,128]{1,0:T(8,128)S(1)}, f32[160,128]{1,0:T(8,128)S(1)}, u32[]{:S(2)}, u32[]{:S(2)}) %collective-permute-start.66) | collective-permute-done | bytes 81952 | tf_op jit(solution)/shard_map/ppermute | solution.py:436
  76.4 0.0 collective-permute-done.67.from_east
  76.4 4.1 %final.1 = (f32[32,16,128]{2,1,0:T(8,128)}, f32[16,128]{1,0:T(8,128)}, f32[2,16,128]{2,1,0:T(8,128)}) custom-call(s32[1]{0:T(128)} %bitcast.lon.lon_ref, s32[2]{0:T(128)S(4)} %get-tuple-element.47.turn_ref, s32[1]{0:T(128)} %bitcast.1.top_ref, f32[32]{0:T(128)} %hmix.3, f32[32,16,128]{2,1,0:T(8,128)S(1)} %get-tuple-element.49.inner, ...), custom_call_target="tpu_custom_call" | custom-call | tf_op jit(solution)/shard_map/final/pallas_call | solution.py:452
Async XLA Ops:
  2.8 20.0 %collective-permute-start.65 = (f32[128,128]{1,0:T(8,128)S(1)}, f32[128,128]{1,0:T(8,128)S(1)}, u32[]{:S(2)}, u32[]{:S(2)}) collective-permute-start(f32[128,128]{1,0:T(8,128)S(1)} %get-tuple-element.53.down), channel_id=1, source_target_pairs={{1,0},{2,1},{3,2},{4,3},{5,4},{6,5},{7,6},{9,8},{10,9},{11,10},{12... | collective-permute-start | bytes 196616 | tf_op jit(solution)/shard_map/ppermute | solution.py:410
  5.3 17.4 %collective-permute-start.64 = (f32[128,128]{1,0:T(8,128)S(1)}, f32[128,128]{1,0:T(8,128)S(1)}, u32[]{:S(2)}, u32[]{:S(2)}) collective-permute-start(f32[128,128]{1,0:T(8,128)S(1)} %get-tuple-element.48.up), channel_id=1, source_target_pairs={{0,1},{1,2},{2,3},{3,4},{4,5},{5,6},{6,7},{8,9},{9,10},{10,11},{11... | collective-permute-start | bytes 196616 | tf_op jit(solution)/shard_map/ppermute | solution.py:409
  6.7 14.1 %collective-permute-start.7 = (f32[128,128]{1,0:T(8,128)S(1)}, f32[128,128]{1,0:T(8,128)}, u32[]{:S(2)}, u32[]{:S(2)}) collective-permute-start(f32[128,128]{1,0:T(8,128)S(1)} %param.3), channel_id=1, source_target_pairs={{39,7},{23,15},{15,23},{7,31},{255,39},{247,47},{239,55},{231,63},... | collective-permute-start | bytes 196616 | tf_op jit(solution)/shard_map/cond/branch_3_fun/ppermute | solution.py:415
  15.5 7.2 %collective-permute-start.6 = (f32[128,128]{1,0:T(8,128)S(1)}, f32[128,128]{1,0:T(8,128)}, u32[]{:S(2)}, u32[]{:S(2)}) collective-permute-start(f32[128,128]{1,0:T(8,128)S(1)} %param.3), channel_id=1, source_target_pairs={{31,7},{15,15},{7,23},{255,31},{247,39},{239,47},{231,55},{223,63}... | collective-permute-start | bytes 196616 | tf_op jit(solution)/shard_map/cond/branch_3_fun/ppermute | solution.py:415
  23.7 52.7 %collective-permute-start.67 = (f32[288,128]{1,0:T(8,128)S(1)}, f32[288,128]{1,0:T(8,128)S(1)}, u32[]{:S(2)}, u32[]{:S(2)}) collective-permute-start(f32[288,128]{1,0:T(8,128)S(1)} %get-tuple-element.58), channel_id=1, source_target_pairs={{8,0},{16,8},{24,16},{32,24},{40,32},{48,40},{56,48},{64,56},{72,6... | collective-permute-start | bytes 442376 | tf_op jit(solution)/shard_map/ppermute | solution.py:437
  59.5 16.9 %collective-permute-start.66 = (f32[160,128]{1,0:T(8,128)S(1)}, f32[160,128]{1,0:T(8,128)S(1)}, u32[]{:S(2)}, u32[]{:S(2)}) collective-permute-start(f32[160,128]{1,0:T(8,128)S(1)} %get-tuple-element.57), channel_id=1, source_target_pairs={{0,8},{8,16},{16,24},{24,32},{32,40},{40,48},{48,56},{56,64},{64,7... | collective-permute-start | bytes 245768 | tf_op jit(solution)/shard_map/ppermute | solution.py:436
